TPU v7x, 512 devices: a whole 4x4x16 slice. The times are simulated.
512 devices in a mesh: section: 4 (over x), expert: 32 (over z, core), dp: 4 (over y).
Axes of the slice: x: 4, y: 4, z: 16, core: 2. Of those that a mesh axis runs over, the one named last changes fastest.
Arguments:
- fwd_input: bfloat16 [4, 256, 2048], P('section', 'dp', 'expert'), may hold values from -6 to 6
- fresh_input: bfloat16 [1, 256, 2048], P(None, 'dp', 'expert'), may hold values from -6 to 6
- fwd_experts: int32 [4, 2, 256, 2], P('section', None, 'dp'), may hold values from 0 to 3, all different within a row; in each aligned block of 64 rows (0 to 63, 64 to 127, ..., all dimensions but the last counted through in order) at most 36 rows name the same one
- fwd_gates: float32 [4, 2, 256, 2], P('section', None, 'dp'), may hold values from 0.2 to 1
- bwd_saved: bfloat16 [4, 2, 256, 2048], P('section', None, 'dp', 'expert'), may hold values from -6 to 6
- bwd_experts: int32 [4, 2, 256, 2], P('section', None, 'dp'), may hold values from 0 to 3, all different within a row; in each aligned block of 64 rows (0 to 63, 64 to 127, ..., all dimensions but the last counted through in order) at most 36 rows name the same one
- bwd_gates: float32 [4, 2, 256, 2], P('section', None, 'dp'), may hold values from 0.2 to 1
- out_grad: bfloat16 [4, 256, 2048], P('section', 'dp', 'expert'), may hold values from -6 to 6
- fresh_grad: bfloat16 [1, 256, 2048], P(None, 'dp', 'expert'), may hold values from -6 to 6
- gate_proj: bfloat16 [4, 4, 7168, 2048], P('section', 'dp', 'expert'), may hold values from -0.125 to 0.125
- down_proj: bfloat16 [4, 4, 7168, 2048], P('section', 'dp', 'expert'), may hold values from -0.0625 to 0.0625
Outputs:
- fwd_output: bfloat16 [4, 2, 256, 2048], P('section', None, 'dp', 'expert')
- input_grad: bfloat16 [4, 2, 256, 2048], P('section', None, 'dp', 'expert')
- gate_grad: bfloat16 [4, 4, 7168, 2048], P('section', 'dp', 'expert')
- down_grad: bfloat16 [4, 4, 7168, 2048], P('section', 'dp', 'expert')
Inputs may be any that keep to these rules, and one draw needn't show every extreme that they name: `fwd_experts`: each token names two different experts. In every aligned block of 64 tokens (one index of dp, one section and step) no expert is named more than 36 times, and in some blocks one expert is named exactly 36 times. `bwd_experts`: each token names two different experts. In every aligned block of 64 tokens (one index of dp, one section and step) no expert is named more than 36 times, and in some blocks one expert is named exactly 36 times.
All inputs are finite; a program needn't handle non-finite values.
Results may differ from a plain program's by a relative error of at most 0.0062.
Values may be sent and summed in bfloat16 or wider, within the bound.
No kernel may reach another device: no remote copies, remote signals or barrier semaphores. Data moves between devices by JAX's collectives and lax.ppermute only.
A program may use at most 64 MiB of HBM per device.

v0:
```python
import math

import jax
import jax.numpy as jnp
from jax import lax
from jax.experimental import pallas as pl
from jax.experimental.pallas import tpu as pltpu
from jax.sharding import Mesh
from jax.sharding import PartitionSpec as P

D = 2048
FF = 7168
EXPERTS = 4
EXPERT = ("z", "core")
BF = jnp.bfloat16
F32 = jnp.float32
CHUNKS = 16
LANES = 128
ROWS = 32
TOKS = EXPERTS * ROWS
HID = 224

NT = (((1,), (1,)), ((), ()))
TN = (((0,), (0,)), ((), ()))


def call(body, outs, *args, scratch=(), limit=32):
    vmem = pl.BlockSpec(memory_space=pltpu.VMEM)
    return pl.pallas_call(
        body,
        out_shape=outs,
        in_specs=[vmem] * len(args),
        out_specs=jax.tree.map(lambda _: vmem, outs),
        scratch_shapes=list(scratch),
        compiler_params=pltpu.CompilerParams(vmem_limit_bytes=limit * 1024 * 1024),
    )(*args)


def shaped(shape, dtype):
    return jax.ShapeDtypeStruct(shape, dtype)


def spread_body(got, weight, out):
    rows = got.shape[1]
    for e in range(EXPERTS):
        scale = weight[e]
        for k in range(CHUNKS):
            out[e, k, 0:ROWS, :] = got[k, 0:ROWS, :]
            out[e, k, ROWS : 2 * ROWS, :] = (scale * got[k, ROWS : 2 * ROWS, :].astype(F32)).astype(BF)
            if rows > 2 * ROWS:
                out[e, k, 2 * ROWS : rows, :] = got[k, 2 * ROWS : rows, :]


def spread(got, weight):
    return call(spread_body, shaped((EXPERTS, *got.shape), BF), got, weight)


def layer_body(stored_at, came, kept, gate_own, gate_other, down_own, down_other, out, own, other, both, grad):
    for e in range(EXPERTS):
        for k in range(CHUNKS):
            lanes = slice(k * LANES, (k + 1) * LANES)
            both[e * ROWS : (e + 1) * ROWS, lanes] = came[e, k, 0:ROWS, :]
            both[TOKS + e * ROWS : TOKS + (e + 1) * ROWS, lanes] = kept[e, k, stored_at : stored_at + ROWS, :]
            grad[e * ROWS : (e + 1) * ROWS, lanes] = came[e, k, ROWS : 2 * ROWS, :]
    tokens, cotangent = both[...], grad[...]
    hidden_fwd, slopes = [], []
    for gate, down, keep in ((gate_own, down_own, own), (gate_other, down_other, other)):
        before = lax.dot_general(tokens, gate[...], NT, preferred_element_type=F32)
        sigmoid = 1.0 / (1.0 + jnp.exp(-before))
        hidden = (before * sigmoid).astype(BF)
        hidden_fwd.append(hidden[0:TOKS])
        through = lax.dot_general(cotangent, down[...], NT, preferred_element_type=F32)
        sig, pre = sigmoid[TOKS:], before[TOKS:]
        slope = (through * sig * (1.0 + pre * (1.0 - sig))).astype(BF)
        slopes.append(slope)
        keep[0] = hidden[TOKS:]
        keep[1] = slope
    forward = jnp.dot(hidden_fwd[0], down_own[...], preferred_element_type=F32) + jnp.dot(
        hidden_fwd[1], down_other[...], preferred_element_type=F32
    )
    backward = jnp.dot(slopes[0], gate_own[...], preferred_element_type=F32) + jnp.dot(
        slopes[1], gate_other[...], preferred_element_type=F32
    )
    forward, backward = forward.astype(BF), backward.astype(BF)
    for e in range(EXPERTS):
        for k in range(CHUNKS):
            rows, lanes = slice(e * ROWS, (e + 1) * ROWS), slice(k * LANES, (k + 1) * LANES)
            out[e, k, 0:ROWS, :] = forward[rows, lanes]
            out[e, k, ROWS : 2 * ROWS, :] = backward[rows, lanes]


def layer(came, kept, stored_at, weights):
    def body(*refs):
        layer_body(stored_at, *refs)

    pair = shaped((2, TOKS, HID), BF)
    return call(
        body,
        (shaped((EXPERTS, CHUNKS, 2 * ROWS, LANES), BF), pair, pair),
        came,
        kept,
        *weights,
        scratch=(pltpu.VMEM((2 * TOKS, D), BF), pltpu.VMEM((TOKS, D), BF)),
    )


def combine_chunks(back, weight, out):
    for k in range(CHUNKS):
        fwd = weight[0] * back[0, k, 0:ROWS, :].astype(F32)
        bwd = back[0, k, ROWS : 2 * ROWS, :].astype(F32)
        for e in range(1, EXPERTS):
            fwd = fwd + weight[e] * back[e, k, 0:ROWS, :].astype(F32)
            bwd = bwd + back[e, k, ROWS : 2 * ROWS, :].astype(F32)
        out[k, 0:ROWS, :] = fwd.astype(BF)
        out[k, ROWS : 2 * ROWS, :] = bwd.astype(BF)


def combine_sum_body(back, weight, squares, out):
    combine_chunks(back, weight, out)
    total = jnp.full((16, LANES), jnp.sum(squares[...]), F32)
    high = total.astype(BF).astype(F32)
    middle = (total - high).astype(BF).astype(F32)
    low = total - high - middle
    row = lax.broadcasted_iota(jnp.int32, (16, LANES), 0)
    zero = jnp.zeros((16, LANES), F32)
    pieces = jnp.where(row == 0, high, jnp.where(row == 1, middle, jnp.where(row == 2, low, zero))).astype(BF)
    for k in range(CHUNKS):
        out[k, 2 * ROWS : 2 * ROWS + 16, :] = pieces


def combine(back, weight, squares=None):
    if squares is None:
        return call(combine_chunks, shaped((CHUNKS, 2 * ROWS, LANES), BF), back, weight)
    return call(combine_sum_body, shaped((CHUNKS, 2 * ROWS + 16, LANES), BF), back, weight, squares)


def grads_body(came0, came0p, came1, came1p, own0, own0p, own1, own1p, gate, down, squares, cot, stored):
    sources = ((came0, came0, 2), (came0p, came0p, 2), (came1, came0, 3), (came1p, came0p, 3))
    for n, (came, kept, at) in enumerate(sources):
        for e in range(EXPERTS):
            for k in range(CHUNKS):
                rows = slice(n * TOKS + e * ROWS, n * TOKS + (e + 1) * ROWS)
                lanes = slice(k * LANES, (k + 1) * LANES)
                cot[rows, lanes] = came[e, k, ROWS : 2 * ROWS, :]
                stored[rows, lanes] = kept[e, k, at * ROWS : (at + 1) * ROWS, :]
    pairs = (own0, own0p, own1, own1p)
    hidden = jnp.concatenate([p[0] for p in pairs], axis=0)
    slope = jnp.concatenate([p[1] for p in pairs], axis=0)
    total = jnp.zeros((8, LANES), F32)
    width = 512
    for at in range(0, D, width):
        lanes = slice(at, at + width)
        for left, right, out in ((slope, stored, gate), (hidden, cot, down)):
            part = lax.dot_general(left, right[:, lanes], TN, preferred_element_type=F32)
            out[:, lanes] = part
            square = jnp.sum((part * part).reshape(HID // 8, 8, width), axis=0)
            for lane in range(0, width, LANES):
                total = total + square[:, lane : lane + LANES]
    squares[...] = total


def grads(*args):
    out = shaped((HID, D), F32)
    tokens = 4 * TOKS
    return call(
        grads_body,
        (out, out, shaped((8, LANES), F32)),
        *args,
        scratch=(pltpu.VMEM((tokens, D), BF), pltpu.VMEM((tokens, D), BF)),
        limit=40,
    )


def swapped(value):
    return lax.ppermute(value, "core", [(0, 1), (1, 0)])


def shifted(value, steps):
    count = lax.axis_size("section")
    return lax.ppermute(
        value, "section", [(s, s + steps) for s in range(max(0, -steps), min(count, count - steps))]
    )


def to_everyone(value, axis):
    return lax.all_to_all(
        jnp.broadcast_to(value[None], (lax.axis_size(axis), *value.shape)), axis, 0, 0, tiled=True
    )


def gate_rows(experts, gate_values):
    half = lax.axis_index("core") * ROWS
    experts = lax.dynamic_slice_in_dim(experts, half, ROWS, 1)
    gate_values = lax.dynamic_slice_in_dim(gate_values, half, ROWS, 1)
    number = jnp.arange(EXPERTS, dtype=jnp.int32)[None, :, None, None]
    rows = jnp.sum(jnp.where(experts[:, None] == number, gate_values[:, None], F32(0.0)), axis=-1)
    return jnp.broadcast_to(rows[..., None], (*rows.shape, LANES))


def on_device(
    fwd_input,
    fresh_input,
    fwd_experts,
    fwd_gates,
    bwd_saved,
    bwd_experts,
    bwd_gates,
    out_grad,
    fresh_grad,
    gate_proj,
    down_proj,
):
    gate_own, down_own = gate_proj[0, 0], down_proj[0, 0]
    section_count = lax.axis_size("section")
    section_index = lax.axis_index("section")
    is_first = section_index == 0
    is_last = section_index == section_count - 1

    streams = jnp.concatenate([fwd_input, out_grad, bwd_saved[0], fresh_input, fresh_grad], axis=0)
    count = streams.shape[0]
    halves = jnp.moveaxis(streams.reshape(count, 2, ROWS, 64), 1, 0)
    met = lax.all_to_all(halves, "core", 0, 0, tiled=True)
    packed = jnp.concatenate([met[0], met[1]], axis=-1)
    first = packed[0:4].reshape(4 * ROWS, LANES)
    fresh = packed[4:6].reshape(2 * ROWS, LANES)

    gate_other, down_other = swapped(gate_own), swapped(down_own)
    weights = (gate_own, gate_other, down_own, down_other)
    fwd_weight = gate_rows(fwd_experts[0], fwd_gates[0])
    bwd_weight = gate_rows(bwd_experts[0], bwd_gates[0])

    got = to_everyone(first, "z")
    came0 = lax.all_to_all(spread(got, bwd_weight[0]), "dp", 0, 0, tiled=True)
    came0p = swapped(came0)
    partial, own0, other0 = layer(came0, came0, 2 * ROWS, weights)
    own0p = swapped(other0)
    back = lax.all_to_all(partial, "dp", 0, 0, tiled=True)
    pieces = lax.all_to_all(combine(back, fwd_weight[0]), "z", 0, 0, tiled=True)
    base = first[0 : 2 * ROWS]
    result0 = (base.astype(F32) + jnp.sum(pieces.astype(F32), axis=0)).astype(BF)

    arriving = shifted(result0[0:ROWS], 1)
    leaving = shifted(result0[ROWS : 2 * ROWS], -1)
    second = jnp.concatenate(
        [
            jnp.where(is_first, fresh[0:ROWS], arriving),
            jnp.where(is_last, fresh[ROWS : 2 * ROWS], leaving),
        ],
        axis=0,
    )

    got = to_everyone(second, "z")
    came1 = lax.all_to_all(spread(got, bwd_weight[1]), "dp", 0, 0, tiled=True)
    came1p = swapped(came1)
    partial, own1, other1 = layer(came1, came0, 3 * ROWS, weights)
    own1p = swapped(other1)
    back = lax.all_to_all(partial, "dp", 0, 0, tiled=True)
    gate_total, down_total, squares = grads(
        came0, came0p, came1, came1p, own0, own0p, own1, own1p
    )
    pieces = lax.all_to_all(combine(back, fwd_weight[1], squares), "z", 0, 0, tiled=True)
    sent = pieces[:, 0 : 2 * ROWS].astype(F32)
    result1 = (second.astype(F32) + jnp.sum(sent, axis=0)).astype(BF)

    along_z = jnp.sum(pieces[:, 2 * ROWS : 2 * ROWS + 3, 0].astype(F32))
    plane = ("section", "dp", "core")
    tiles = lax.all_to_all(
        jnp.full((32, 8, LANES), along_z, F32), plane, 0, 0, tiled=True
    )
    total = jnp.sum(tiles[:, 0, 0])
    clip_limit = 0.25 * math.sqrt(2.0 * section_count * EXPERTS * FF * D)
    factor = clip_limit / jnp.maximum(jnp.sqrt(total), clip_limit)
    gate_grad = (gate_total * factor).astype(BF)[None, None]
    down_grad = (down_total * factor).astype(BF)[None, None]

    results = jnp.stack([result0, result1]).reshape(2, 2, ROWS, 2, 64)
    homed = lax.all_to_all(jnp.moveaxis(results, 3, 0), "core", 0, 0, tiled=True)
    final = jnp.transpose(homed, (2, 1, 0, 3, 4)).reshape(2, 1, 2, 2 * ROWS, 64)
    return (final[0], final[1], gate_grad, down_grad)


def solution(mesh):
    split = Mesh(
        mesh.devices.reshape(mesh.shape["section"], CHUNKS, 2, mesh.shape["dp"]),
        ("section", "z", "core", "dp"),
    )
    return jax.shard_map(
        on_device,
        mesh=split,
        in_specs=(
            P("section", "dp", EXPERT),
            P(None, "dp", EXPERT),
            P("section", None, "dp", None),
            P("section", None, "dp", None),
            P("section", None, "dp", EXPERT),
            P("section", None, "dp", None),
            P("section", None, "dp", None),
            P("section", "dp", EXPERT),
            P(None, "dp", EXPERT),
            P("section", "dp", EXPERT, None),
            P("section", "dp", EXPERT, None),
        ),
        out_specs=(
            P("section", None, "dp", EXPERT),
            P("section", None, "dp", EXPERT),
            P("section", "dp", EXPERT, None),
            P("section", "dp", EXPERT, None),
        ),
        check_vma=False,
    )
```

profile of v0, /device:TPU:1, one launch (start us, length us, event | category | flops | bytes accessed | tf_op | source)
XLA Modules:
  0.0 268.8 jit_solution(15810127265895420896)
XLA Ops:
  0.7 0.7 constant_dynamic-update-slice_fusion.3
  1.4 0.7 constant_dynamic-update-slice_fusion.2
  2.1 0.8 copy_dynamic-update-slice_fusion
  2.9 0.7 constant_dynamic-update-slice_fusion.1
  3.6 0.7 constant_dynamic-update-slice_fusion
  4.5 10.3 %all_to_all.55 = bf16[2,2,6144]{2,1,0:T(2,128)(2,1)S(1)} all-to-all(bf16[2,2,6144]{2,1,0:T(2,128)(2,1)S(1)} %reshape.113), channel_id=1, replica_groups=mesh['section'=4,'z'=16,'core'=2,'dp'=4] {'core'}, dimensions={0} | all-to-all | bytes 98304 | tf_op jit(solution)/shard_map/all_to_all | solution.py:222
  15.0 0.9 broadcast_in_dim.75
  15.9 9.6 %all-to-all-start.1 = ((bf16[16,128,128]{2,1,0:T(8,128)(2,1)}), bf16[16,128,128]{2,1,0:T(8,128)(2,1)S(1)}, u32[]{:S(2)}, u32[]{:S(2)}) async-start(bf16[16,128,128]{2,1,0:T(8,128)(2,1)} %broadcast_in_dim.75), calls=%async_computation.1 | async-start | bytes 1048576 | tf_op jit(solution)/shard_map/all_to_all | solution.py:186
  26.3 21.9 %all-to-all-done.1.got = bf16[16,128,128]{2,1,0:T(8,128)(2,1)S(1)} async-done(((bf16[16,128,128]{2,1,0:T(8,128)(2,1)}), bf16[16,128,128]{2,1,0:T(8,128)(2,1)S(1)}, u32[]{:S(2)}, u32[]{:S(2)}) %all-to-all-start.1) | async-done | bytes 524320 | tf_op jit(solution)/shard_map/all_to_all | solution.py:186
  48.4 1.3 copy-done
  49.8 4.3 %all-to-all-start.2 = ((bf16[4,16,128,128]{3,2,1,0:T(8,128)(2,1)}), bf16[4,16,128,128]{3,2,1,0:T(8,128)(2,1)S(1)}, u32[]{:S(2)}, u32[]{:S(2)}) async-start(bf16[4,16,128,128]{3,2,1,0:T(8,128)(2,1)} %copy-done), calls=%async_computation.2 | async-start | bytes 4194304 | tf_op jit(solution)/shard_map/all_to_all | solution.py:233
  54.1 9.3 %collective-permute-start = (bf16[224,2048]{1,0:T(8,128)(2,1)S(1)}, bf16[224,2048]{1,0:T(8,128)(2,1)S(1)}, u32[]{:S(2)}, u32[]{:S(2)}) collective-permute-start(bf16[224,2048]{1,0:T(8,128)(2,1)S(1)} %bitcast.62), channel_id=1, source_target_pairs={{0,4},{4,0},{1,5},{5,1},{2,6},{6,2},{3,7},{7,3},{8,12},{12,8},{9,1... | collective-permute-start | bytes 2752520 | tf_op jit(solution)/shard_map/ppermute | solution.py:175
  63.4 1.9 collective-permute-start.1
  65.5 0.9 copy-done.5
  66.4 1.6 collective-permute-done.1.refs_5_
  68.0 0.9 copy-done.8
  68.9 3.9 %all-to-all-done.2.refs_0_.refs_1_.came0 = bf16[4,16,128,128]{3,2,1,0:T(8,128)(2,1)S(1)} async-done(((bf16[4,16,128,128]{3,2,1,0:T(8,128)(2,1)}), bf16[4,16,128,128]{3,2,1,0:T(8,128)(2,1)S(1)}, u32[]{:S(2)}, u32[]{:S(2)}) %all-to-all-start.2) | async-done | bytes 2097184 | tf_op jit(solution)/shard_map/all_to_all | solution.py:233
  72.8 1.2 copy-done.3
  74.0 1.2 copy-done.6
  75.2 1.2 copy-done.9
  76.4 1.9 shard_map.139
  78.3 1.0 copy-done.15
  79.3 3.5 %all-to-all-start.3 = ((bf16[4,16,64,128]{3,2,1,0:T(8,128)(2,1)}), bf16[4,16,64,128]{3,2,1,0:T(8,128)(2,1)S(1)}, u32[]{:S(2)}, u32[]{:S(2)}) async-start(bf16[4,16,64,128]{3,2,1,0:T(8,128)(2,1)} %copy-done.15), calls=%async_computation.3 | async-start | bytes 2097152 | tf_op jit(solution)/shard_map/all_to_all | solution.py:237
  83.4 9.1 %all-to-all-done.3.back = bf16[4,16,64,128]{3,2,1,0:T(8,128)(2,1)S(1)} async-done(((bf16[4,16,64,128]{3,2,1,0:T(8,128)(2,1)}), bf16[4,16,64,128]{3,2,1,0:T(8,128)(2,1)S(1)}, u32[]{:S(2)}, u32[]{:S(2)}) %all-to-all-start.3) | async-done | bytes 1048608 | tf_op jit(solution)/shard_map/all_to_all | solution.py:237
  92.6 0.9 shard_map.140
  93.5 23.6 %all-to-all-start.4 = ((bf16[16,64,128]{2,1,0:T(8,128)(2,1)}), bf16[16,64,128]{2,1,0:T(8,128)(2,1)S(1)}, u32[]{:S(2)}, u32[]{:S(2)}) async-start(bf16[16,64,128]{2,1,0:T(8,128)(2,1)} %shard_map.140), calls=%async_computation.4 | async-start | bytes 524288 | tf_op jit(solution)/shard_map/all_to_all | solution.py:238
  117.1 12.6 %all-to-all-done.4 = bf16[16,64,128]{2,1,0:T(8,128)(2,1)S(1)} async-done(((bf16[16,64,128]{2,1,0:T(8,128)(2,1)}), bf16[16,64,128]{2,1,0:T(8,128)(2,1)S(1)}, u32[]{:S(2)}, u32[]{:S(2)}) %all-to-all-start.4) | async-done | bytes 262176 | tf_op jit(solution)/shard_map/all_to_all | solution.py:238
  129.9 3.1 %collective-permute-start.2 = (bf16[32,128]{1,0:T(8,128)(2,1)S(1)}, bf16[32,128]{1,0:T(8,128)(2,1)S(1)}, u32[]{:S(2)}, u32[]{:S(2)}) collective-permute-start(bf16[32,128]{1,0:T(8,128)(2,1)S(1)} %get-tuple-element.28), channel_id=1, source_target_pairs={{0,128},{128,256},{256,384},{1,129},{129,257},{257,385},{2,130},{1... | collective-permute-start | bytes 24584 | tf_op jit(solution)/shard_map/ppermute | solution.py:180
  133.0 1.3 collective-permute-start.3
  134.3 3.1 %collective-permute-done.3 = bf16[32,128]{1,0:T(8,128)(2,1)S(1)} collective-permute-done((bf16[32,128]{1,0:T(8,128)(2,1)S(1)}, bf16[32,128]{1,0:T(8,128)(2,1)S(1)}, u32[]{:S(2)}, u32[]{:S(2)}) %collective-permute-start.3) | collective-permute-done | bytes 8224 | tf_op jit(solution)/shard_map/ppermute | solution.py:180
  137.5 0.8 broadcast_in_dim.85
  138.2 10.7 %all-to-all-start.5 = ((bf16[16,64,128]{2,1,0:T(8,128)(2,1)}), bf16[16,64,128]{2,1,0:T(8,128)(2,1)S(1)}, u32[]{:S(2)}, u32[]{:S(2)}) async-start(bf16[16,64,128]{2,1,0:T(8,128)(2,1)} %broadcast_in_dim.85), calls=%async_computation.5 | async-start | bytes 524288 | tf_op jit(solution)/shard_map/all_to_all | solution.py:186
  149.0 5.0 %collective-permute-start.4 = (bf16[4,16,128,128]{3,2,1,0:T(8,128)(2,1)S(1)}, bf16[4,16,128,128]{3,2,1,0:T(8,128)(2,1)}, u32[]{:S(2)}, u32[]{:S(2)}) collective-permute-start(bf16[4,16,128,128]{3,2,1,0:T(8,128)(2,1)S(1)} %all-to-all-done.2.refs_0_.refs_1_.came0), channel_id=1, source_target_pairs={{0,4},{4,0},{1,5},{5,1},{2,6},{6,2},{3,7},{7,3},{8,12},{12,8},{9,1... | collective-permute-start | bytes 6291464 | tf_op jit(solution)/shard_map/ppermute | solution.py:175
  154.0 7.7 %all-to-all-done.5.got = bf16[16,64,128]{2,1,0:T(8,128)(2,1)S(1)} async-done(((bf16[16,64,128]{2,1,0:T(8,128)(2,1)}), bf16[16,64,128]{2,1,0:T(8,128)(2,1)S(1)}, u32[]{:S(2)}, u32[]{:S(2)}) %all-to-all-start.5) | async-done | bytes 262176 | tf_op jit(solution)/shard_map/all_to_all | solution.py:186
  161.7 0.7 broadcast_in_dim.87.weight
  162.6 12.2 %all_to_all.56.refs_0_.came1 = bf16[4,16,64,128]{3,2,1,0:T(8,128)(2,1)S(1)} all-to-all(bf16[4,16,64,128]{3,2,1,0:T(8,128)(2,1)S(1)} %shard_map.141), channel_id=1, replica_groups=mesh['section'=4,'z'=16,'core'=2,'dp'=4] {'dp'}, dimensions={0} | all-to-all | bytes 2097152 | tf_op jit(solution)/shard_map/all_to_all | solution.py:253
  174.8 9.9 %collective-permute-start.5 = (bf16[4,16,64,128]{3,2,1,0:T(8,128)(2,1)S(1)}, bf16[4,16,64,128]{3,2,1,0:T(8,128)(2,1)}, u32[]{:S(2)}, u32[]{:S(2)}) collective-permute-start(bf16[4,16,64,128]{3,2,1,0:T(8,128)(2,1)S(1)} %all_to_all.56.refs_0_.came1), channel_id=1, source_target_pairs={{0,4},{4,0},{1,5},{5,1},{2,6},{6,2},{3,7},{7,3},{8,12},{12,8},{9,1... | collective-permute-start | bytes 3145736 | tf_op jit(solution)/shard_map/ppermute | solution.py:175
  184.7 1.2 copy-done.2
  185.8 1.2 copy-done.4
  187.0 1.2 copy-done.7
  188.2 1.2 copy-done.10
  189.4 1.9 shard_map.142
  191.3 1.0 copy-done.14
  192.3 0.7 copy-done.16
  193.0 4.2 %all-to-all-start.7 = ((bf16[4,16,64,128]{3,2,1,0:T(8,128)(2,1)}), bf16[4,16,64,128]{3,2,1,0:T(8,128)(2,1)}, u32[]{:S(2)}, u32[]{:S(2)}) async-start(bf16[4,16,64,128]{3,2,1,0:T(8,128)(2,1)} %copy-done.14), calls=%async_computation.7 | async-start | bytes 2097152 | tf_op jit(solution)/shard_map/all_to_all | solution.py:257
  197.2 1.9 collective-permute-start.6
  199.2 2.4 collective-permute-start.7
  201.6 1.2 collective-permute-done.7.own1p
  202.8 3.1 %shard_map.143 = (f32[224,2048]{1,0:T(8,128)S(1)}, f32[224,2048]{1,0:T(8,128)S(1)}, f32[8,128]{1,0:T(8,128)S(1)}) custom-call(bf16[4,16,128,128]{3,2,1,0:T(8,128)(2,1)S(1)} %all-to-all-done.2.refs_0_.refs_1_.came0, bf16[4,16,128,128]{3,2,1,0:T(8,128)(2,1)} %collective-permute-done.4.came0p, bf16[4,16,64,128]{3,2,1,0:T(8,128)(2,1)S(1)} %all_to_all.56.refs_0_.came1, ...), custom_call_target="tpu_custom_call" | custom-call | tf_op jit(solution)/shard_map/pallas_call | solution.py:29
  205.9 1.3 copy-done.11
  207.2 1.2 copy-done.13
  208.4 4.1 %all-to-all-done.7.back = bf16[4,16,64,128]{3,2,1,0:T(8,128)(2,1)} async-done(((bf16[4,16,64,128]{3,2,1,0:T(8,128)(2,1)}), bf16[4,16,64,128]{3,2,1,0:T(8,128)(2,1)}, u32[]{:S(2)}, u32[]{:S(2)}) %all-to-all-start.7) | async-done | bytes 1048608 | tf_op jit(solution)/shard_map/all_to_all | solution.py:257
  212.5 2.2 shard_map.144
  214.7 7.9 %all-to-all-start.8 = ((bf16[16,80,128]{2,1,0:T(8,128)(2,1)}), bf16[16,80,128]{2,1,0:T(8,128)(2,1)S(1)}, u32[]{:S(2)}, u32[]{:S(2)}) async-start(bf16[16,80,128]{2,1,0:T(8,128)(2,1)} %shard_map.144), calls=%async_computation.8 | async-start | bytes 655360 | tf_op jit(solution)/shard_map/all_to_all | solution.py:261
  223.0 14.7 %all-to-all-done.8 = bf16[16,80,128]{2,1,0:T(8,128)(2,1)S(1)} async-done(((bf16[16,80,128]{2,1,0:T(8,128)(2,1)}), bf16[16,80,128]{2,1,0:T(8,128)(2,1)S(1)}, u32[]{:S(2)}, u32[]{:S(2)}) %all-to-all-start.8) | async-done | bytes 327712 | tf_op jit(solution)/shard_map/all_to_all | solution.py:261
  238.1 0.7 reshape.115
  238.8 9.8 %all-to-all-start.9 = ((bf16[2,2,4096]{2,1,0:T(2,128)(2,1)}), bf16[2,2,4096]{2,1,0:T(2,128)(2,1)S(1)}, u32[]{:S(2)}, u32[]{:S(2)}) async-start(bf16[2,2,4096]{2,1,0:T(2,128)(2,1)} %reshape.115), calls=%async_computation.9 | async-start | bytes 65536 | tf_op jit(solution)/shard_map/all_to_all | solution.py:277
  249.6 1.3 broadcast_in_dim.90
  250.9 5.1 %all-to-all-start.10 = ((f32[32,8,128]{2,1,0:T(8,128)}), f32[32,8,128]{2,1,0:T(8,128)S(1)}, u32[]{:S(2)}, u32[]{:S(2)}) async-start(f32[32,8,128]{2,1,0:T(8,128)} %broadcast_in_dim.90), calls=%async_computation.10 | async-start | bytes 262144 | tf_op jit(solution)/shard_map/all_to_all | solution.py:267
  256.2 0.6 fusion.11
  256.8 6.9 %all-to-all-done.10 = f32[32,8,128]{2,1,0:T(8,128)S(1)} async-done(((f32[32,8,128]{2,1,0:T(8,128)}), f32[32,8,128]{2,1,0:T(8,128)S(1)}, u32[]{:S(2)}, u32[]{:S(2)}) %all-to-all-start.10) | async-done | bytes 131104 | tf_op jit(solution)/shard_map/all_to_all | solution.py:267
  263.7 0.6 slice_reduce_fusion
  265.1 2.6 fusion.1
  267.7 1.1 fusion
  (77 shorter events, 4.5 us)
Async XLA Ops:
  0.6 24.8 %copy-start.22 = (f32[1,2,64,2]{2,3,1,0:T(2,128)S(1)}, f32[1,2,64,2]{2,3,1,0:T(2,128)}, u32[]{:S(2)}) copy-start(f32[1,2,64,2]{2,3,1,0:T(2,128)} %param.14) | copy-start | bytes 3076
  0.6 24.8 %copy-start.23 = (f32[1,2,64,2]{2,3,1,0:T(2,128)S(1)}, f32[1,2,64,2]{2,3,1,0:T(2,128)}, u32[]{:S(2)}) copy-start(f32[1,2,64,2]{2,3,1,0:T(2,128)} %param.17) | copy-start | bytes 3076
  0.7 24.9 %copy-start.24 = (s32[1,2,64,2]{2,3,1,0:T(2,128)S(1)}, s32[1,2,64,2]{2,3,1,0:T(2,128)}, u32[]{:S(2)}) copy-start(s32[1,2,64,2]{2,3,1,0:T(2,128)} %param.13) | copy-start | bytes 3076
  0.7 24.9 %copy-start.25 = (s32[1,2,64,2]{2,3,1,0:T(2,128)S(1)}, s32[1,2,64,2]{2,3,1,0:T(2,128)}, u32[]{:S(2)}) copy-start(s32[1,2,64,2]{2,3,1,0:T(2,128)} %param.16) | copy-start | bytes 3076
  15.9 32.3 %all-to-all-start.1 = ((bf16[16,128,128]{2,1,0:T(8,128)(2,1)}), bf16[16,128,128]{2,1,0:T(8,128)(2,1)S(1)}, u32[]{:S(2)}, u32[]{:S(2)}) async-start(bf16[16,128,128]{2,1,0:T(8,128)(2,1)} %broadcast_in_dim.75), calls=%async_computation.1 | async-start | bytes 1048576 | tf_op jit(solution)/shard_map/all_to_all | solution.py:186
  48.4 1.4 copy-start
  49.8 4.3 %copy-start.1 = (bf16[1,1,224,2048]{3,2,1,0:T(8,128)(2,1)S(1)}, bf16[1,1,224,2048]{3,2,1,0:T(8,128)(2,1)}, u32[]{:S(2)}) copy-start(bf16[1,1,224,2048]{3,2,1,0:T(8,128)(2,1)} %param.20) | copy-start | bytes 2752516
  49.8 23.1 %all-to-all-start.2 = ((bf16[4,16,128,128]{3,2,1,0:T(8,128)(2,1)}), bf16[4,16,128,128]{3,2,1,0:T(8,128)(2,1)S(1)}, u32[]{:S(2)}, u32[]{:S(2)}) async-start(bf16[4,16,128,128]{3,2,1,0:T(8,128)(2,1)} %copy-done), calls=%async_computation.2 | async-start | bytes 4194304 | tf_op jit(solution)/shard_map/all_to_all | solution.py:233
  54.1 11.4 %collective-permute-start = (bf16[224,2048]{1,0:T(8,128)(2,1)S(1)}, bf16[224,2048]{1,0:T(8,128)(2,1)S(1)}, u32[]{:S(2)}, u32[]{:S(2)}) collective-permute-start(bf16[224,2048]{1,0:T(8,128)(2,1)S(1)} %bitcast.62), channel_id=1, source_target_pairs={{0,4},{4,0},{1,5},{5,1},{2,6},{6,2},{3,7},{7,3},{8,12},{12,8},{9,1... | collective-permute-start | bytes 2752520 | tf_op jit(solution)/shard_map/ppermute | solution.py:175
  63.4 4.6 %collective-permute-start.1 = (bf16[224,2048]{1,0:T(8,128)(2,1)}, bf16[224,2048]{1,0:T(8,128)(2,1)S(1)}, u32[]{:S(2)}, u32[]{:S(2)}) collective-permute-start(bf16[224,2048]{1,0:T(8,128)(2,1)} %bitcast.65), channel_id=1, source_target_pairs={{0,4},{4,0},{1,5},{5,1},{2,6},{6,2},{3,7},{7,3},{8,12},{12,8},{9,1... | collective-permute-start | bytes 2752520 | tf_op jit(solution)/shard_map/ppermute | solution.py:175
  65.5 0.9 copy-start.5
  68.0 0.9 copy-start.8
  72.8 1.2 copy-start.3
  74.0 1.2 copy-start.6
  75.2 1.2 copy-start.9
  78.3 1.0 copy-start.15
  79.3 13.2 %all-to-all-start.3 = ((bf16[4,16,64,128]{3,2,1,0:T(8,128)(2,1)}), bf16[4,16,64,128]{3,2,1,0:T(8,128)(2,1)S(1)}, u32[]{:S(2)}, u32[]{:S(2)}) async-start(bf16[4,16,64,128]{3,2,1,0:T(8,128)(2,1)} %copy-done.15), calls=%async_computation.3 | async-start | bytes 2097152 | tf_op jit(solution)/shard_map/all_to_all | solution.py:237
  93.5 36.3 %all-to-all-start.4 = ((bf16[16,64,128]{2,1,0:T(8,128)(2,1)}), bf16[16,64,128]{2,1,0:T(8,128)(2,1)S(1)}, u32[]{:S(2)}, u32[]{:S(2)}) async-start(bf16[16,64,128]{2,1,0:T(8,128)(2,1)} %shard_map.140), calls=%async_computation.4 | async-start | bytes 524288 | tf_op jit(solution)/shard_map/all_to_all | solution.py:238
  117.1 45.3 %copy-start.19 = (f32[2,32,128]{2,1,0:T(8,128)}, f32[2,32,128]{2,1,0:T(8,128)S(1)}, u32[]{:S(2)}) copy-start(f32[2,32,128]{2,1,0:T(8,128)S(1)} %fusion.5) | copy-start | bytes 98308
  129.8 44.9 %copy-start.17 = (f32[64,128]{1,0:T(8,128)}, f32[64,128]{1,0:T(8,128)S(1)}, u32[]{:S(2)}) copy-start(f32[64,128]{1,0:T(8,128)S(1)} %convert_reduce_fusion.1) | copy-start | bytes 98308
  129.9 4.4 %collective-permute-start.2 = (bf16[32,128]{1,0:T(8,128)(2,1)S(1)}, bf16[32,128]{1,0:T(8,128)(2,1)S(1)}, u32[]{:S(2)}, u32[]{:S(2)}) collective-permute-start(bf16[32,128]{1,0:T(8,128)(2,1)S(1)} %get-tuple-element.28), channel_id=1, source_target_pairs={{0,128},{128,256},{256,384},{1,129},{129,257},{257,385},{2,130},{1... | collective-permute-start | bytes 24584 | tf_op jit(solution)/shard_map/ppermute | solution.py:180
  133.0 4.4 %collective-permute-start.3 = (bf16[32,128]{1,0:T(8,128)(2,1)S(1)}, bf16[32,128]{1,0:T(8,128)(2,1)S(1)}, u32[]{:S(2)}, u32[]{:S(2)}) collective-permute-start(bf16[32,128]{1,0:T(8,128)(2,1)S(1)} %get-tuple-element.29), channel_id=1, source_target_pairs={{128,0},{256,128},{384,256},{129,1},{257,129},{385,257},{130,2},{2... | collective-permute-start | bytes 24584 | tf_op jit(solution)/shard_map/ppermute | solution.py:180
  138.2 23.5 %all-to-all-start.5 = ((bf16[16,64,128]{2,1,0:T(8,128)(2,1)}), bf16[16,64,128]{2,1,0:T(8,128)(2,1)S(1)}, u32[]{:S(2)}, u32[]{:S(2)}) async-start(bf16[16,64,128]{2,1,0:T(8,128)(2,1)} %broadcast_in_dim.85), calls=%async_computation.5 | async-start | bytes 524288 | tf_op jit(solution)/shard_map/all_to_all | solution.py:186
  149.0 52.6 %collective-permute-start.4 = (bf16[4,16,128,128]{3,2,1,0:T(8,128)(2,1)S(1)}, bf16[4,16,128,128]{3,2,1,0:T(8,128)(2,1)}, u32[]{:S(2)}, u32[]{:S(2)}) collective-permute-start(bf16[4,16,128,128]{3,2,1,0:T(8,128)(2,1)S(1)} %all-to-all-done.2.refs_0_.refs_1_.came0), channel_id=1, source_target_pairs={{0,4},{4,0},{1,5},{5,1},{2,6},{6,2},{3,7},{7,3},{8,12},{12,8},{9,1... | collective-permute-start | bytes 6291464 | tf_op jit(solution)/shard_map/ppermute | solution.py:175
  174.8 28.0 %collective-permute-start.5 = (bf16[4,16,64,128]{3,2,1,0:T(8,128)(2,1)S(1)}, bf16[4,16,64,128]{3,2,1,0:T(8,128)(2,1)}, u32[]{:S(2)}, u32[]{:S(2)}) collective-permute-start(bf16[4,16,64,128]{3,2,1,0:T(8,128)(2,1)S(1)} %all_to_all.56.refs_0_.came1), channel_id=1, source_target_pairs={{0,4},{4,0},{1,5},{5,1},{2,6},{6,2},{3,7},{7,3},{8,12},{12,8},{9,1... | collective-permute-start | bytes 3145736 | tf_op jit(solution)/shard_map/ppermute | solution.py:175
  184.7 1.2 copy-start.2
  185.8 1.2 copy-start.4
  187.0 1.2 copy-start.7
  188.2 1.2 copy-start.10
  191.3 1.0 copy-start.14
  192.3 0.7 copy-start.16
  193.0 19.5 %all-to-all-start.7 = ((bf16[4,16,64,128]{3,2,1,0:T(8,128)(2,1)}), bf16[4,16,64,128]{3,2,1,0:T(8,128)(2,1)}, u32[]{:S(2)}, u32[]{:S(2)}) async-start(bf16[4,16,64,128]{3,2,1,0:T(8,128)(2,1)} %copy-done.14), calls=%async_computation.7 | async-start | bytes 2097152 | tf_op jit(solution)/shard_map/all_to_all | solution.py:257
  197.2 4.3 %collective-permute-start.6 = (bf16[2,128,224]{2,1,0:T(8,128)(2,1)S(1)}, bf16[2,128,224]{2,1,0:T(8,128)(2,1)S(1)}, u32[]{:S(2)}, u32[]{:S(2)}) collective-permute-start(bf16[2,128,224]{2,1,0:T(8,128)(2,1)S(1)} %get-tuple-element.16), channel_id=1, source_target_pairs={{0,4},{4,0},{1,5},{5,1},{2,6},{6,2},{3,7},{7,3},{8,12},{12,8},{9,1... | collective-permute-start | bytes 344072 | tf_op jit(solution)/shard_map/ppermute | solution.py:175
  199.2 3.6 %collective-permute-start.7 = (bf16[2,128,224]{2,1,0:T(8,128)(2,1)}, bf16[2,128,224]{2,1,0:T(8,128)(2,1)S(1)}, u32[]{:S(2)}, u32[]{:S(2)}) collective-permute-start(bf16[2,128,224]{2,1,0:T(8,128)(2,1)} %copy-done.16), channel_id=1, source_target_pairs={{0,4},{4,0},{1,5},{5,1},{2,6},{6,2},{3,7},{7,3},{8,12},{12,8},{9,1... | collective-permute-start | bytes 344072 | tf_op jit(solution)/shard_map/ppermute | solution.py:175
  202.8 9.7 %copy-start.21 = (f32[4,32]{1,0:T(4,128)S(1)}, f32[4,32]{1,0:T(4,128)}, u32[]{:S(2)}) copy-start(f32[4,32]{1,0:T(4,128)} %get-tuple-element.30) | copy-start | bytes 1540
  205.9 1.3 copy-start.11
  207.2 1.2 copy-start.13
  208.4 14.2 %copy-start.20 = (f32[2,32,128]{2,1,0:T(8,128)S(1)}, f32[2,32,128]{2,1,0:T(8,128)}, u32[]{:S(2)}) copy-start(f32[2,32,128]{2,1,0:T(8,128)} %copy-done.19) | copy-start | bytes 98308
  208.4 14.3 %copy-start.18 = (f32[64,128]{1,0:T(8,128)S(1)}, f32[64,128]{1,0:T(8,128)}, u32[]{:S(2)}) copy-start(f32[64,128]{1,0:T(8,128)} %copy-done.17) | copy-start | bytes 98308
  214.7 23.0 %all-to-all-start.8 = ((bf16[16,80,128]{2,1,0:T(8,128)(2,1)}), bf16[16,80,128]{2,1,0:T(8,128)(2,1)S(1)}, u32[]{:S(2)}, u32[]{:S(2)}) async-start(bf16[16,80,128]{2,1,0:T(8,128)(2,1)} %shard_map.144), calls=%async_computation.8 | async-start | bytes 655360 | tf_op jit(solution)/shard_map/all_to_all | solution.py:261
  238.1 29.6 %copy-start.12 = (f32[224,2048]{1,0:T(8,128)S(1)}, f32[224,2048]{1,0:T(8,128)}, u32[]{:S(2)}) copy-start(f32[224,2048]{1,0:T(8,128)} %copy-done.11) | copy-start | bytes 5505028
  238.8 10.8 %all-to-all-start.9 = ((bf16[2,2,4096]{2,1,0:T(2,128)(2,1)}), bf16[2,2,4096]{2,1,0:T(2,128)(2,1)S(1)}, u32[]{:S(2)}, u32[]{:S(2)}) async-start(bf16[2,2,4096]{2,1,0:T(2,128)(2,1)} %reshape.115), calls=%async_computation.9 | async-start | bytes 65536 | tf_op jit(solution)/shard_map/all_to_all | solution.py:277
  250.9 12.8 %all-to-all-start.10 = ((f32[32,8,128]{2,1,0:T(8,128)}), f32[32,8,128]{2,1,0:T(8,128)S(1)}, u32[]{:S(2)}, u32[]{:S(2)}) async-start(f32[32,8,128]{2,1,0:T(8,128)} %broadcast_in_dim.90), calls=%async_computation.10 | async-start | bytes 262144 | tf_op jit(solution)/shard_map/all_to_all | solution.py:267
where the time goes:
time: 271 us; the launch traced here: 269 us
  starting transfers between devices  114 us (42%)
  waiting for transfers between devices  87.5 us (32%)
  local copies, waits for them, and re-layouts  27.7 us (10%)
  blocking collectives  22.4 us (8%)
  Pallas kernels  10.3 us (4%)
  other arithmetic  5.46 us (2%)
    ppermute x6, starting transfers between devices, swapped(): return lax.ppermute(value, 'core', [(0, 1), (1, 0)])  30.4 us
    all_to_all x2, waiting for transfers between devices, to_everyone(): lax.all_to_all(jnp.broadcast_to(value[None], (lax.axis_size(axis), *value...  29.7 us
    all_to_all x1, starting transfers between devices, on_device(): pieces = lax.all_to_all(combine(back, fwd_weight[0]), 'z', 0, 0, tiled=True)  23.6 us
    unnamed x60, local copies, waits for them, and re-layouts  20.7 us
    all_to_all x2, starting transfers between devices, to_everyone(): lax.all_to_all(jnp.broadcast_to(value[None], (lax.axis_size(axis), *value...  20.3 us
    all_to_all x1, waiting for transfers between devices, on_device(): lax.all_to_all(combine(back, fwd_weight[1], squares), 'z', 0, 0, tiled=True)  14.7 us
    all_to_all x2, waiting for transfers between devices, on_device(): back = lax.all_to_all(partial, 'dp', 0, 0, tiled=True)  13.2 us
    all_to_all x1, waiting for transfers between devices, on_device(): pieces = lax.all_to_all(combine(back, fwd_weight[0]), 'z', 0, 0, tiled=True)  12.6 us
  transfers between devices with their start and end apart: 17, of which 13 were waited for; matrix products, arithmetic and copies ran while one was open for 1% of the time, Pallas kernels for 2%

commit v1 on v0

v1 whole, which is shorter than its diff:
```python
import math

import jax
import jax.numpy as jnp
from jax import lax
from jax.experimental import pallas as pl
from jax.experimental.pallas import tpu as pltpu
from jax.sharding import Mesh
from jax.sharding import PartitionSpec as P

D = 2048
FF = 7168
EXPERTS = 4
EXPERT = ("z", "core")
BF = jnp.bfloat16
F32 = jnp.float32
CHUNKS = 16
LANES = 128
ROWS = 32
TOKS = EXPERTS * ROWS
HID = 224

NT = (((1,), (1,)), ((), ()))
TN = (((0,), (0,)), ((), ()))


VMEM, HBM, SMEM = pltpu.VMEM, pltpu.HBM, pltpu.SMEM


def call(body, outs, args, scratch=(), limit=24):
    return pl.pallas_call(
        body,
        out_shape=tuple(jax.ShapeDtypeStruct(shape, dtype) for shape, dtype, _ in outs),
        in_specs=[pl.BlockSpec(memory_space=space) for _, space in args],
        out_specs=tuple(pl.BlockSpec(memory_space=space) for _, _, space in outs),
        scratch_shapes=list(scratch),
        compiler_params=pltpu.CompilerParams(vmem_limit_bytes=limit * 1024 * 1024),
    )(*(array for array, _ in args))


def sems(number):
    return pltpu.SemaphoreType.DMA((number,))


def halves(first, own, other):
    return jnp.where(first, jnp.concatenate([own, other], -1), jnp.concatenate([other, own], -1))


def pack_body(core, *refs):
    inputs, (send, keep) = refs[:-2], refs[-2:]
    mine = pl.multiple_of(core[0] * ROWS, ROWS)
    others = pl.multiple_of((1 - core[0]) * ROWS, ROWS)
    at = 0
    for ref in inputs:
        for n in range(ref.shape[0]):
            keep[at] = ref[n, pl.ds(mine, ROWS), :]
            send[at] = ref[n, pl.ds(others, ROWS), :]
            at += 1


def pack(core, arrays):
    count = sum(a.shape[0] for a in arrays)
    shape = (count, ROWS, 64)
    return call(
        pack_body,
        ((shape, BF, VMEM), (shape, BF, VMEM)),
        ((core, SMEM), *((a, VMEM) for a in arrays)),
    )


def open_body(core, keep, got, out, first, fresh, arrived):
    lead = jnp.full((ROWS, LANES), core[0], jnp.int32) == 0
    for n in range(6):
        rows = halves(lead, keep[n].astype(F32), got[n].astype(F32)).astype(BF)
        if n < 4:
            first[n * ROWS : (n + 1) * ROWS, :] = rows
        else:
            fresh[(n - 4) * ROWS : (n - 3) * ROWS, :] = rows
    copies = [pltpu.make_async_copy(first, out.at[k], arrived.at[k]) for k in range(CHUNKS)]
    for c in copies:
        c.start()
    for c in copies:
        c.wait()


def opened(core, keep, got):
    return call(
        open_body,
        (
            ((CHUNKS, 4 * ROWS, LANES), BF, HBM),
            ((4 * ROWS, LANES), BF, VMEM),
            ((2 * ROWS, LANES), BF, VMEM),
        ),
        ((core, SMEM), (keep, VMEM), (got, VMEM)),
        scratch=(sems(CHUNKS),),
    )


def next_body(place, arriving, leaving, fresh, out, second, arrived):
    at_first = jnp.full((ROWS, LANES), place[0], jnp.int32) == 0
    at_last = jnp.full((ROWS, LANES), place[1], jnp.int32) == 0
    second[0:ROWS, :] = jnp.where(at_first, fresh[0:ROWS, :].astype(F32), arriving[...].astype(F32)).astype(BF)
    second[ROWS : 2 * ROWS, :] = jnp.where(
        at_last, fresh[ROWS : 2 * ROWS, :].astype(F32), leaving[...].astype(F32)
    ).astype(BF)
    copies = [pltpu.make_async_copy(second, out.at[k], arrived.at[k]) for k in range(CHUNKS)]
    for c in copies:
        c.start()
    for c in copies:
        c.wait()


def following(place, arriving, leaving, fresh):
    return call(
        next_body,
        (((CHUNKS, 2 * ROWS, LANES), BF, HBM), ((2 * ROWS, LANES), BF, VMEM)),
        ((place, SMEM), (arriving, VMEM), (leaving, VMEM), (fresh, VMEM)),
        scratch=(sems(CHUNKS),),
    )


def spread_body(got, weight, out, staged, sent):
    rows = got.shape[1]
    copies = []
    for e in range(EXPERTS):
        scale = weight[e]
        for k in range(CHUNKS):
            staged[e, k, 0:ROWS, :] = got[k, 0:ROWS, :]
            staged[e, k, ROWS : 2 * ROWS, :] = (scale * got[k, ROWS : 2 * ROWS, :].astype(F32)).astype(BF)
            if rows > 2 * ROWS:
                staged[e, k, 2 * ROWS : rows, :] = got[k, 2 * ROWS : rows, :]
        copies.append(pltpu.make_async_copy(staged.at[e], out.at[e], sent.at[e]))
        copies[-1].start()
    for c in copies:
        c.wait()


def spread(got, weight):
    shape = (EXPERTS, *got.shape)
    return call(
        spread_body,
        ((shape, BF, HBM),),
        ((got, VMEM), (weight, VMEM)),
        scratch=(pltpu.VMEM(shape, BF), sems(EXPERTS)),
    )[0]


def layer_body(kept_at, came, *refs):
    refs = list(refs)
    kept = refs.pop(0) if kept_at is not None else None
    gate_own, gate_other, down_own, down_other, out, own, other = refs[:7]
    both, grad, staged, g_own, g_other, d_own, d_other, sent, loaded = refs[7:16]
    loads = [
        pltpu.make_async_copy(s, d, loaded.at[n])
        for n, (s, d) in enumerate(
            ((gate_own, g_own), (down_own, d_own), (gate_other, g_other), (down_other, d_other))
        )
    ]
    if kept_at is not None:
        stored = refs[16]
        loads.append(
            pltpu.make_async_copy(kept.at[:, :, pl.ds(kept_at, ROWS), :], stored, loaded.at[4])
        )
        loads[4].start()
    for c in loads[0:4]:
        c.start()
    for e in range(EXPERTS):
        for k in range(CHUNKS):
            lanes = slice(k * LANES, (k + 1) * LANES)
            both[e * ROWS : (e + 1) * ROWS, lanes] = came[e, k, 0:ROWS, :]
            grad[e * ROWS : (e + 1) * ROWS, lanes] = came[e, k, ROWS : 2 * ROWS, :]
            if kept_at is None:
                both[TOKS + e * ROWS : TOKS + (e + 1) * ROWS, lanes] = came[e, k, 2 * ROWS : 3 * ROWS, :]
    if kept_at is not None:
        loads[4].wait()
        for e in range(EXPERTS):
            for k in range(CHUNKS):
                lanes = slice(k * LANES, (k + 1) * LANES)
                both[TOKS + e * ROWS : TOKS + (e + 1) * ROWS, lanes] = stored[e, k]
    tokens, cotangent = both[...], grad[...]
    hidden_fwd, slopes = [], []
    for n, (gate, down, keep) in enumerate(((g_own, d_own, own), (g_other, d_other, other))):
        loads[2 * n].wait()
        before = lax.dot_general(tokens, gate[...], NT, preferred_element_type=F32)
        sigmoid = 1.0 / (1.0 + jnp.exp(-before))
        hidden = (before * sigmoid).astype(BF)
        hidden_fwd.append(hidden[0:TOKS])
        loads[2 * n + 1].wait()
        through = lax.dot_general(cotangent, down[...], NT, preferred_element_type=F32)
        sig, pre = sigmoid[TOKS:], before[TOKS:]
        slope = (through * sig * (1.0 + pre * (1.0 - sig))).astype(BF)
        slopes.append(slope)
        keep[0] = hidden[TOKS:]
        keep[1] = slope
    forward = jnp.dot(hidden_fwd[0], d_own[...], preferred_element_type=F32) + jnp.dot(
        hidden_fwd[1], d_other[...], preferred_element_type=F32
    )
    backward = jnp.dot(slopes[0], g_own[...], preferred_element_type=F32) + jnp.dot(
        slopes[1], g_other[...], preferred_element_type=F32
    )
    forward, backward = forward.astype(BF), backward.astype(BF)
    stores = []
    for e in range(EXPERTS):
        for k in range(CHUNKS):
            rows, lanes = slice(e * ROWS, (e + 1) * ROWS), slice(k * LANES, (k + 1) * LANES)
            staged[e, k, 0:ROWS, :] = forward[rows, lanes]
            staged[e, k, ROWS : 2 * ROWS, :] = backward[rows, lanes]
        stores.append(pltpu.make_async_copy(staged.at[e], out.at[e], sent.at[e]))
        stores[-1].start()
    for c in stores:
        c.wait()


def layer(came, kept, kept_at, weights):
    def body(*refs):
        layer_body(kept_at, *refs)

    shape = (EXPERTS, CHUNKS, 2 * ROWS, LANES)
    pair = (2, TOKS, HID)
    weight = pltpu.VMEM((HID, D), BF)
    scratch = [
        pltpu.VMEM((2 * TOKS, D), BF),
        pltpu.VMEM((TOKS, D), BF),
        pltpu.VMEM(shape, BF),
        *([weight] * 4),
        sems(EXPERTS),
        sems(5),
    ]
    args = [(came, VMEM)]
    if kept_at is not None:
        scratch.append(pltpu.VMEM((EXPERTS, CHUNKS, ROWS, LANES), BF))
        args.append((kept, HBM))
    return call(
        body,
        ((shape, BF, HBM), (pair, BF, VMEM), (pair, BF, VMEM)),
        (*args, *((w, HBM) for w in weights)),
        scratch=scratch,
    )


def combine_chunks(back, weight, out):
    for k in range(CHUNKS):
        fwd = weight[0] * back[0, k, 0:ROWS, :].astype(F32)
        bwd = back[0, k, ROWS : 2 * ROWS, :].astype(F32)
        for e in range(1, EXPERTS):
            fwd = fwd + weight[e] * back[e, k, 0:ROWS, :].astype(F32)
            bwd = bwd + back[e, k, ROWS : 2 * ROWS, :].astype(F32)
        out[k, 0:ROWS, :] = fwd.astype(BF)
        out[k, ROWS : 2 * ROWS, :] = bwd.astype(BF)


def combine_body(back, weight, out, staged, sent):
    combine_chunks(back, weight, staged)
    c = pltpu.make_async_copy(staged, out, sent.at[0])
    c.start()
    c.wait()


def combine_sum_body(back, weight, squares, out, staged, sent):
    combine_chunks(back, weight, staged)
    total = jnp.full((16, LANES), jnp.sum(squares[...]), F32)
    high = total.astype(BF).astype(F32)
    middle = (total - high).astype(BF).astype(F32)
    low = total - high - middle
    row = lax.broadcasted_iota(jnp.int32, (16, LANES), 0)
    zero = jnp.zeros((16, LANES), F32)
    pieces = jnp.where(row == 0, high, jnp.where(row == 1, middle, jnp.where(row == 2, low, zero))).astype(BF)
    for k in range(CHUNKS):
        staged[k, 2 * ROWS : 2 * ROWS + 16, :] = pieces
    c = pltpu.make_async_copy(staged, out, sent.at[0])
    c.start()
    c.wait()


def combine(back, weight, squares=None):
    shape = (CHUNKS, 2 * ROWS + (16 if squares is not None else 0), LANES)
    args = [(back, VMEM), (weight, VMEM)]
    if squares is not None:
        args.append((squares, VMEM))
    return call(
        combine_body if squares is None else combine_sum_body,
        ((shape, BF, HBM),),
        args,
        scratch=(pltpu.VMEM(shape, BF), sems(1)),
    )[0]


def grads_body(
    came0, came0p, came1, came1p, own0, own0p, own1, own1p, gate, down, squares,
    buf0, buf0p, buf1, buf1p, cot, stored, gate_v, down_v, loaded, sent,
):
    tail = pl.ds(ROWS, 3 * ROWS)
    one = pl.ds(ROWS, ROWS)
    loads = [
        pltpu.make_async_copy(came0.at[:, :, tail, :], buf0, loaded.at[0]),
        pltpu.make_async_copy(came0p.at[:, :, tail, :], buf0p, loaded.at[1]),
        pltpu.make_async_copy(came1.at[:, :, one, :], buf1, loaded.at[2]),
        pltpu.make_async_copy(came1p.at[:, :, one, :], buf1p, loaded.at[3]),
    ]
    for c in loads:
        c.start()
    sources = ((buf0, buf0, 1), (buf0p, buf0p, 1), (buf1, buf0, 2), (buf1p, buf0p, 2))
    for n, (came, kept, at) in enumerate(sources):
        loads[n].wait()
        for e in range(EXPERTS):
            for k in range(CHUNKS):
                rows = slice(n * TOKS + e * ROWS, n * TOKS + (e + 1) * ROWS)
                lanes = slice(k * LANES, (k + 1) * LANES)
                cot[rows, lanes] = came[e, k, 0:ROWS, :]
                stored[rows, lanes] = kept[e, k, at * ROWS : (at + 1) * ROWS, :]
    pairs = (own0, own0p, own1, own1p)
    hidden = jnp.concatenate([p[0] for p in pairs], axis=0)
    slope = jnp.concatenate([p[1] for p in pairs], axis=0)
    total = jnp.zeros((8, LANES), F32)
    width = 512
    stores = []
    for n, at in enumerate(range(0, D, width)):
        lanes = slice(at, at + width)
        for m, (left, right, out, held) in enumerate(
            ((slope, stored, gate, gate_v), (hidden, cot, down, down_v))
        ):
            part = lax.dot_general(left, right[:, lanes], TN, preferred_element_type=F32)
            held[:, lanes] = part
            stores.append(
                pltpu.make_async_copy(
                    held.at[:, pl.ds(at, width)], out.at[:, pl.ds(at, width)], sent.at[2 * n + m]
                )
            )
            stores[-1].start()
            square = jnp.sum((part * part).reshape(HID // 8, 8, width), axis=0)
            for lane in range(0, width, LANES):
                total = total + square[:, lane : lane + LANES]
    squares[...] = total
    for c in stores:
        c.wait()


def grads(cames, owns):
    tokens = 4 * TOKS
    total = ((HID, D), F32, HBM)
    return call(
        grads_body,
        (total, total, ((8, LANES), F32, VMEM)),
        (*((c, HBM) for c in cames), *((o, VMEM) for o in owns)),
        scratch=(
            pltpu.VMEM((EXPERTS, CHUNKS, 3 * ROWS, LANES), BF),
            pltpu.VMEM((EXPERTS, CHUNKS, 3 * ROWS, LANES), BF),
            pltpu.VMEM((EXPERTS, CHUNKS, ROWS, LANES), BF),
            pltpu.VMEM((EXPERTS, CHUNKS, ROWS, LANES), BF),
            pltpu.VMEM((tokens, D), BF),
            pltpu.VMEM((tokens, D), BF),
            pltpu.VMEM((HID, D), F32),
            pltpu.VMEM((HID, D), F32),
            sems(4),
            sems(8),
        ),
    )


def close_body(pieces, base, result, tiles):
    total = base[...].astype(F32)
    extra = jnp.zeros((16, LANES), F32)
    for k in range(CHUNKS):
        total = total + pieces[k, 0 : 2 * ROWS, :].astype(F32)
        extra = extra + pieces[k, 2 * ROWS : 2 * ROWS + 16, :].astype(F32)
    result[...] = total.astype(BF)
    along = jnp.sum(extra, axis=0, keepdims=True)
    for k in range(tiles.shape[0]):
        tiles[k] = jnp.broadcast_to(along, (8, LANES))


def closed(pieces, base, count):
    return call(
        close_body,
        (((2 * ROWS, LANES), BF, VMEM), ((count, 8, LANES), F32, VMEM)),
        ((pieces, VMEM), (base, VMEM)),
    )


STEP = 32


def clip_body(limit, tiles, gate, down, gate_out, down_out, gate_v, down_v, gate_o, down_o, loaded, sent):
    work = [
        (held, kept, out, pl.ds(at, STEP), pltpu.make_async_copy(
            source.at[pl.ds(at, STEP)], held.at[pl.ds(at, STEP)], loaded.at[m * (HID // STEP) + n]
        ))
        for n, at in enumerate(range(0, HID, STEP))
        for m, (source, held, kept, out) in enumerate(
            ((gate, gate_v, gate_o, gate_out), (down, down_v, down_o, down_out))
        )
    ]
    for *_, c in work:
        c.start()
    total = jnp.sum(tiles[...], axis=0)
    factor = (limit / jnp.maximum(jnp.sqrt(total), limit))[0:1, 0:1]
    stores = []
    for n, (held, kept, out, rows, c) in enumerate(work):
        c.wait()
        kept[rows, :] = (held[rows, :] * factor).astype(BF)
        stores.append(pltpu.make_async_copy(kept.at[rows], out.at[rows], sent.at[n]))
        stores[-1].start()
    for c in stores:
        c.wait()


def clipped(limit, tiles, gate, down):
    def body(*refs):
        clip_body(limit, *refs)

    number = 2 * (HID // STEP)
    out = ((HID, D), BF, HBM)
    return call(
        body,
        (out, out),
        ((tiles, VMEM), (gate, HBM), (down, HBM)),
        scratch=(
            pltpu.VMEM((HID, D), F32),
            pltpu.VMEM((HID, D), F32),
            pltpu.VMEM((HID, D), BF),
            pltpu.VMEM((HID, D), BF),
            sems(number),
            sems(number),
        ),
    )


def swapped(value):
    return lax.ppermute(value, "core", [(0, 1), (1, 0)])


def shifted(value, steps):
    count = lax.axis_size("section")
    return lax.ppermute(
        value, "section", [(s, s + steps) for s in range(max(0, -steps), min(count, count - steps))]
    )


def lanes_home(result, first):
    rows = result.reshape(2, ROWS, 2, 64)
    low, high = rows[:, :, 0], rows[:, :, 1]
    got = swapped(jnp.where(first, high, low))
    mine = jnp.where(first, low, high)
    return jnp.where(first, jnp.concatenate([mine, got], 1), jnp.concatenate([got, mine], 1))


def gate_rows(experts, gate_values):
    half = lax.axis_index("core") * ROWS
    experts = lax.dynamic_slice_in_dim(experts, half, ROWS, 1)
    gate_values = lax.dynamic_slice_in_dim(gate_values, half, ROWS, 1)
    number = jnp.arange(EXPERTS, dtype=jnp.int32)[None, :, None, None]
    rows = jnp.sum(jnp.where(experts[:, None] == number, gate_values[:, None], F32(0.0)), axis=-1)
    return jnp.broadcast_to(rows[..., None], (*rows.shape, LANES))


def on_device(
    fwd_input,
    fresh_input,
    fwd_experts,
    fwd_gates,
    bwd_saved,
    bwd_experts,
    bwd_gates,
    out_grad,
    fresh_grad,
    gate_proj,
    down_proj,
):
    gate_own, down_own = gate_proj[0, 0], down_proj[0, 0]
    section_count = lax.axis_size("section")
    section_index = lax.axis_index("section")

    core_index = lax.axis_index("core").astype(jnp.int32)
    core = core_index[None]
    place = jnp.stack([section_index, section_count - 1 - section_index]).astype(jnp.int32)

    send, keep = pack(core, (fwd_input, out_grad, bwd_saved[0], fresh_input, fresh_grad))
    outgoing, first, fresh = opened(core, keep, swapped(send))

    weights = (gate_own, swapped(gate_own), down_own, swapped(down_own))
    fwd_weight = gate_rows(fwd_experts[0], fwd_gates[0])
    bwd_weight = gate_rows(bwd_experts[0], bwd_gates[0])

    got = lax.all_to_all(outgoing, "z", 0, 0, tiled=True)
    came0 = lax.all_to_all(spread(got, bwd_weight[0]), "dp", 0, 0, tiled=True)
    partial, own0, other0 = layer(came0, None, None, weights)
    came0, partial = lax.optimization_barrier((came0, partial))
    came0p, own0p = swapped(came0), swapped(other0)
    back = lax.all_to_all(partial, "dp", 0, 0, tiled=True)
    pieces = lax.all_to_all(combine(back, fwd_weight[0]), "z", 0, 0, tiled=True)
    base = first[0 : 2 * ROWS]
    result0 = (base.astype(F32) + jnp.sum(pieces.astype(F32), axis=0)).astype(BF)

    arriving = shifted(result0[0:ROWS], 1)
    leaving = shifted(result0[ROWS : 2 * ROWS], -1)
    outgoing, second = following(place, arriving, leaving, fresh)

    got = lax.all_to_all(outgoing, "z", 0, 0, tiled=True)
    came1 = lax.all_to_all(spread(got, bwd_weight[1]), "dp", 0, 0, tiled=True)
    partial, own1, other1 = layer(came1, came0, 3 * ROWS, weights)
    came1, partial = lax.optimization_barrier((came1, partial))
    came1p, own1p = swapped(came1), swapped(other1)
    back = lax.all_to_all(partial, "dp", 0, 0, tiled=True)
    gate_total, down_total, squares = grads(
        (came0, came0p, came1, came1p), (own0, own0p, own1, own1p)
    )
    pieces = lax.all_to_all(combine(back, fwd_weight[1], squares), "z", 0, 0, tiled=True)

    plane = ("section", "dp", "core")
    result1, tiles = closed(pieces, second, 32)
    tiles = lax.all_to_all(tiles, plane, 0, 0, tiled=True)
    clip_limit = 0.25 * math.sqrt(2.0 * section_count * EXPERTS * FF * D)
    gate_grad, down_grad = clipped(clip_limit, tiles, gate_total, down_total)

    leads = core_index == 0
    home0, home1 = lanes_home(result0, leads), lanes_home(result1, leads)
    fwd_output = jnp.stack([home0[0], home1[0]])[None]
    input_grad = jnp.stack([home0[1], home1[1]])[None]
    return (fwd_output, input_grad, gate_grad[None, None], down_grad[None, None])


def solution(mesh):
    split = Mesh(
        mesh.devices.reshape(mesh.shape["section"], CHUNKS, 2, mesh.shape["dp"]),
        ("section", "z", "core", "dp"),
    )
    return jax.shard_map(
        on_device,
        mesh=split,
        in_specs=(
            P("section", "dp", EXPERT),
            P(None, "dp", EXPERT),
            P("section", None, "dp", None),
            P("section", None, "dp", None),
            P("section", None, "dp", EXPERT),
            P("section", None, "dp", None),
            P("section", None, "dp", None),
            P("section", "dp", EXPERT),
            P(None, "dp", EXPERT),
            P("section", "dp", EXPERT, None),
            P("section", "dp", EXPERT, None),
        ),
        out_specs=(
            P("section", None, "dp", EXPERT),
            P("section", None, "dp", EXPERT),
            P("section", "dp", EXPERT, None),
            P("section", "dp", EXPERT, None),
        ),
        check_vma=False,
    )
```

time: 271 us -> 271 us (level)
  Pallas kernels: 10.3 us -> 23.7 us
  blocking collectives: 22.4 us -> 12.2 us
  starting transfers between devices: 114 us -> 124 us
  waiting for transfers between devices: 87.5 us -> 81.7 us
  other arithmetic: 5.46 us -> 1.45 us
  local copies, waits for them, and re-layouts: 27.7 us -> 24.5 us
    ppermute x6 -> x9, starting transfers between devices: 30.4 us -> 50.7 us  [swapped(): return lax.ppermute(value, 'core', [(0, 1), (1, 0)])]
    pallas_call x7 -> x12, Pallas kernels: 10.3 us -> 23.7 us  [call(): pl.pallas_call(body, out_shape=tuple((jax.ShapeDtypeStruct(shape, dtype)...]
    all_to_all x1 -> x0, blocking collectives: 10.3 us -> none  [on_device(): met = lax.all_to_all(halves, 'core', 0, 0, tiled=True)]
    all_to_all x4 -> x3, starting transfers between devices: 35.2 us -> 25.7 us  [the longest x2 20.3 us: on_device(): got = lax.all_to_all(outgoing, 'z', 0, 0, tiled=True)]
    all_to_all x1, waiting for transfers between devices: 14.7 us -> 11.1 us  [on_device(): lax.all_to_all(combine(back, fwd_weight[1], squares), 'z', 0, 0, tiled=True)]
    broadcast_in_dim x3 -> x0, local copies, waits for them, and re-layouts: 2.97 us -> none  [the longest x2 1.66 us: to_everyone(): jnp.broadcast_to(value[None], (lax.axis_size(axis), *value.shape))]
    all_to_all x4 -> x3, waiting for transfers between devices: 37 us -> 35.3 us  [the longest x2 28.9 us: on_device(): got = lax.all_to_all(outgoing, 'z', 0, 0, tiled=True)]
    unnamed x60 -> x52, local copies, waits for them, and re-layouts: 20.7 us -> 21.8 us
  transfers between devices with their start and end apart: 17 -> 19, of which waited for: 13 -> 14; matrix products, arithmetic and copies ran while one was open for 1% -> 1% of each run, Pallas kernels for 2% -> 4%
where the time goes in v1:
time: 271 us; the launch traced here: 269 us
  starting transfers between devices  124 us (46%)
  waiting for transfers between devices  81.7 us (30%)
  local copies, waits for them, and re-layouts  24.5 us (9%)
  Pallas kernels  23.7 us (9%)
  blocking collectives  12.2 us (5%)
    ppermute x9, starting transfers between devices, swapped(): return lax.ppermute(value, 'core', [(0, 1), (1, 0)])  50.7 us
    all_to_all x2, waiting for transfers between devices, on_device(): got = lax.all_to_all(outgoing, 'z', 0, 0, tiled=True)  28.9 us
    pallas_call x12, Pallas kernels, call(): pl.pallas_call(body, out_shape=tuple((jax.ShapeDtypeStruct(shape, dtype)...  23.7 us
    all_to_all x1, starting transfers between devices, on_device(): pieces = lax.all_to_all(combine(back, fwd_weight[0]), 'z', 0, 0, tiled=True)  23.6 us
    unnamed x52, local copies, waits for them, and re-layouts  21.8 us
    all_to_all x2, starting transfers between devices, on_device(): got = lax.all_to_all(outgoing, 'z', 0, 0, tiled=True)  20.3 us
    all_to_all x1, waiting for transfers between devices, on_device(): pieces = lax.all_to_all(combine(back, fwd_weight[0]), 'z', 0, 0, tiled=True)  12.7 us
    all_to_all x1, blocking collectives, on_device(): came1 = lax.all_to_all(spread(got, bwd_weight[1]), 'dp', 0, 0, tiled=True)  12.2 us
  transfers between devices with their start and end apart: 19, of which 14 were waited for; matrix products, arithmetic and copies ran while one was open for 1% of the time, Pallas kernels for 4%

profile of v1, /device:TPU:1, one launch (start us, length us, event | category | flops | bytes accessed | tf_op | source)
XLA Modules:
  0.0 268.9 jit_solution(26227762337349472)
XLA Ops:
  0.6 0.7 copy-done.17
  1.4 0.7 copy-done.18
  2.1 0.7 copy-done.19
  2.8 0.7 copy-done.20
  3.6 0.7 copy-done.21
  4.3 8.7 %collective-permute-start = (bf16[6,32,64]{2,1,0:T(8,128)(2,1)S(1)}, bf16[6,32,64]{2,1,0:T(8,128)(2,1)S(1)}, u32[]{:S(2)}, u32[]{:S(2)}) collective-permute-start(bf16[6,32,64]{2,1,0:T(8,128)(2,1)S(1)} %get-tuple-element.29), channel_id=1, source_target_pairs={{0,4},{4,0},{1,5},{5,1},{2,6},{6,2},{3,7},{7,3},{8,12},{12,8},{9,1... | collective-permute-start | bytes 73736 | tf_op jit(solution)/shard_map/ppermute | solution.py:429
  13.0 0.9 collective-permute-done.got
  13.9 1.0 shard_map.139
  14.9 9.6 %all-to-all-start = ((bf16[16,128,128]{2,1,0:T(8,128)(2,1)}), bf16[16,128,128]{2,1,0:T(8,128)(2,1)S(1)}, u32[]{:S(2)}, u32[]{:S(2)}) async-start(bf16[16,128,128]{2,1,0:T(8,128)(2,1)} %get-tuple-element.31), calls=%async_computation | async-start | bytes 1048576 | tf_op jit(solution)/shard_map/all_to_all | solution.py:484
  24.5 0.8 dynamic-slice_bitcast_fusion
  25.3 0.8 dynamic-slice_bitcast_fusion.1
  26.1 21.2 %all-to-all-done.got = bf16[16,128,128]{2,1,0:T(8,128)(2,1)S(1)} async-done(((bf16[16,128,128]{2,1,0:T(8,128)(2,1)}), bf16[16,128,128]{2,1,0:T(8,128)(2,1)S(1)}, u32[]{:S(2)}, u32[]{:S(2)}) %all-to-all-start) | async-done | bytes 524320 | tf_op jit(solution)/shard_map/all_to_all | solution.py:484
  47.7 1.3 copy-done
  49.0 4.3 %all-to-all-start.1 = ((bf16[4,16,128,128]{3,2,1,0:T(8,128)(2,1)}), bf16[4,16,128,128]{3,2,1,0:T(8,128)(2,1)S(1)}, u32[]{:S(2)}, u32[]{:S(2)}) async-start(bf16[4,16,128,128]{3,2,1,0:T(8,128)(2,1)} %copy-done), calls=%async_computation.1 | async-start | bytes 4194304 | tf_op jit(solution)/shard_map/all_to_all | solution.py:485
  53.4 9.3 %collective-permute-start.1 = (bf16[224,2048]{1,0:T(8,128)(2,1)S(1)}, bf16[224,2048]{1,0:T(8,128)(2,1)S(1)}, u32[]{:S(2)}, u32[]{:S(2)}) collective-permute-start(bf16[224,2048]{1,0:T(8,128)(2,1)S(1)} %bitcast.36), channel_id=1, source_target_pairs={{0,4},{4,0},{1,5},{5,1},{2,6},{6,2},{3,7},{7,3},{8,12},{12,8},{9,1... | collective-permute-start | bytes 2752520 | tf_op jit(solution)/shard_map/ppermute | solution.py:429
  62.6 1.9 collective-permute-start.2
  64.7 0.9 copy-done.5
  65.6 1.6 collective-permute-done.2.refs_4_.refs_5_
  67.2 0.9 copy-done.8
  68.1 3.9 %all-to-all-done.1.refs_0_.refs_1_.came0 = bf16[4,16,128,128]{3,2,1,0:T(8,128)(2,1)S(1)} async-done(((bf16[4,16,128,128]{3,2,1,0:T(8,128)(2,1)}), bf16[4,16,128,128]{3,2,1,0:T(8,128)(2,1)S(1)}, u32[]{:S(2)}, u32[]{:S(2)}) %all-to-all-start.1) | async-done | bytes 2097184 | tf_op jit(solution)/shard_map/all_to_all | solution.py:485
  72.1 1.2 copy-done.3
  73.3 1.2 copy-done.6
  74.5 1.2 copy-done.9
  75.6 4.8 %shard_map.141 = (bf16[4,16,64,128]{3,2,1,0:T(8,128)(2,1)S(1)}, bf16[2,128,224]{2,1,0:T(8,128)(2,1)S(1)}, bf16[2,128,224]{2,1,0:T(8,128)(2,1)S(1)}) custom-call(bf16[4,16,128,128]{3,2,1,0:T(8,128)(2,1)S(1)} %all-to-all-done.1.refs_0_.refs_1_.came0, bf16[224,2048]{1,0:T(8,128)(2,1)S(1)} %bitcast.37, bf16[224,2048]{1,0:T(8,128)(2,1)S(1)} %copy-done.6, ...), custom_call_target="tpu_custom_call" | custom-call | tf_op jit(solution)/shard_map/pallas_call | solution.py:31
  80.5 1.0 copy-done.16
  81.5 3.5 %all-to-all-start.2 = ((bf16[4,16,64,128]{3,2,1,0:T(8,128)(2,1)}), bf16[4,16,64,128]{3,2,1,0:T(8,128)(2,1)S(1)}, u32[]{:S(2)}, u32[]{:S(2)}) async-start(bf16[4,16,64,128]{3,2,1,0:T(8,128)(2,1)} %copy-done.16), calls=%async_computation.2 | async-start | bytes 2097152 | tf_op jit(solution)/shard_map/all_to_all | solution.py:489
  85.6 9.1 %all-to-all-done.2.back = bf16[4,16,64,128]{3,2,1,0:T(8,128)(2,1)S(1)} async-done(((bf16[4,16,64,128]{3,2,1,0:T(8,128)(2,1)}), bf16[4,16,64,128]{3,2,1,0:T(8,128)(2,1)S(1)}, u32[]{:S(2)}, u32[]{:S(2)}) %all-to-all-start.2) | async-done | bytes 1048608 | tf_op jit(solution)/shard_map/all_to_all | solution.py:489
  94.8 0.9 shard_map.142
  95.7 23.6 %all-to-all-start.3 = ((bf16[16,64,128]{2,1,0:T(8,128)(2,1)}), bf16[16,64,128]{2,1,0:T(8,128)(2,1)S(1)}, u32[]{:S(2)}, u32[]{:S(2)}) async-start(bf16[16,64,128]{2,1,0:T(8,128)(2,1)} %shard_map.142), calls=%async_computation.3 | async-start | bytes 524288 | tf_op jit(solution)/shard_map/all_to_all | solution.py:490
  119.3 12.7 %all-to-all-done.3 = bf16[16,64,128]{2,1,0:T(8,128)(2,1)S(1)} async-done(((bf16[16,64,128]{2,1,0:T(8,128)(2,1)}), bf16[16,64,128]{2,1,0:T(8,128)(2,1)S(1)}, u32[]{:S(2)}, u32[]{:S(2)}) %all-to-all-start.3) | async-done | bytes 262176 | tf_op jit(solution)/shard_map/all_to_all | solution.py:490
  132.1 3.1 %collective-permute-start.4 = (bf16[32,128]{1,0:T(8,128)(2,1)S(1)}, bf16[32,128]{1,0:T(8,128)(2,1)S(1)}, u32[]{:S(2)}, u32[]{:S(2)}) collective-permute-start(bf16[32,128]{1,0:T(8,128)(2,1)S(1)} %get-tuple-element.65), channel_id=1, source_target_pairs={{0,128},{128,256},{256,384},{1,129},{129,257},{257,385},{2,130},{1... | collective-permute-start | bytes 24584 | tf_op jit(solution)/shard_map/ppermute | solution.py:434
  135.2 1.3 collective-permute-start.5
  136.6 3.0 %collective-permute-done.5.leaving = bf16[32,128]{1,0:T(8,128)(2,1)S(1)} collective-permute-done((bf16[32,128]{1,0:T(8,128)(2,1)S(1)}, bf16[32,128]{1,0:T(8,128)(2,1)S(1)}, u32[]{:S(2)}, u32[]{:S(2)}) %collective-permute-start.5) | collective-permute-done | bytes 8224 | tf_op jit(solution)/shard_map/ppermute | solution.py:434
  139.6 1.4 shard_map.143
  141.1 10.7 %all-to-all-start.4 = ((bf16[16,64,128]{2,1,0:T(8,128)(2,1)}), bf16[16,64,128]{2,1,0:T(8,128)(2,1)S(1)}, u32[]{:S(2)}, u32[]{:S(2)}) async-start(bf16[16,64,128]{2,1,0:T(8,128)(2,1)} %get-tuple-element.35), calls=%async_computation.4 | async-start | bytes 524288 | tf_op jit(solution)/shard_map/all_to_all | solution.py:498
  151.8 5.0 %collective-permute-start.6 = (bf16[4,16,128,128]{3,2,1,0:T(8,128)(2,1)S(1)}, bf16[4,16,128,128]{3,2,1,0:T(8,128)(2,1)}, u32[]{:S(2)}, u32[]{:S(2)}) collective-permute-start(bf16[4,16,128,128]{3,2,1,0:T(8,128)(2,1)S(1)} %all-to-all-done.1.refs_0_.refs_1_.came0), channel_id=1, source_target_pairs={{0,4},{4,0},{1,5},{5,1},{2,6},{6,2},{3,7},{7,3},{8,12},{12,8},{9,1... | collective-permute-start | bytes 6291464 | tf_op jit(solution)/shard_map/ppermute | solution.py:429
  156.8 7.7 %all-to-all-done.4.got = bf16[16,64,128]{2,1,0:T(8,128)(2,1)S(1)} async-done(((bf16[16,64,128]{2,1,0:T(8,128)(2,1)}), bf16[16,64,128]{2,1,0:T(8,128)(2,1)S(1)}, u32[]{:S(2)}, u32[]{:S(2)}) %all-to-all-start.4) | async-done | bytes 262176 | tf_op jit(solution)/shard_map/all_to_all | solution.py:498
  164.8 12.2 %all_to_all.45.refs_0_.came1 = bf16[4,16,64,128]{3,2,1,0:T(8,128)(2,1)S(1)} all-to-all(bf16[4,16,64,128]{3,2,1,0:T(8,128)(2,1)S(1)} %shard_map.144), channel_id=1, replica_groups=mesh['section'=4,'z'=16,'core'=2,'dp'=4] {'dp'}, dimensions={0} | all-to-all | bytes 2097152 | tf_op jit(solution)/shard_map/all_to_all | solution.py:499
  177.0 1.2 copy-done.2
  178.2 1.2 copy-done.4
  179.4 1.2 copy-done.7
  180.6 1.2 copy-done.10
  181.7 4.9 %shard_map.145 = (bf16[4,16,64,128]{3,2,1,0:T(8,128)(2,1)S(1)}, bf16[2,128,224]{2,1,0:T(8,128)(2,1)S(1)}, bf16[2,128,224]{2,1,0:T(8,128)(2,1)S(1)}) custom-call(bf16[4,16,64,128]{3,2,1,0:T(8,128)(2,1)S(1)} %all_to_all.45.refs_0_.came1, bf16[4,16,128,128]{3,2,1,0:T(8,128)(2,1)S(1)} %all-to-all-done.1.refs_0_.refs_1_.came0, bf16[224,2048]{1,0:T(8,128)(2,1)S(1)} %bitcast.38, ...), custom_call_target="tpu_custom_call" | custom-call | tf_op jit(solution)/shard_map/pallas_call | solution.py:31
  186.7 1.0 copy-done.15
  188.3 9.9 %collective-permute-start.7 = (bf16[4,16,64,128]{3,2,1,0:T(8,128)(2,1)S(1)}, bf16[4,16,64,128]{3,2,1,0:T(8,128)(2,1)}, u32[]{:S(2)}, u32[]{:S(2)}) collective-permute-start(bf16[4,16,64,128]{3,2,1,0:T(8,128)(2,1)S(1)} %all_to_all.45.refs_0_.came1), channel_id=1, source_target_pairs={{0,4},{4,0},{1,5},{5,1},{2,6},{6,2},{3,7},{7,3},{8,12},{12,8},{9,1... | collective-permute-start | bytes 3145736 | tf_op jit(solution)/shard_map/ppermute | solution.py:429
  198.2 4.3 %all-to-all-start.6 = ((bf16[4,16,64,128]{3,2,1,0:T(8,128)(2,1)}), bf16[4,16,64,128]{3,2,1,0:T(8,128)(2,1)}, u32[]{:S(2)}, u32[]{:S(2)}) async-start(bf16[4,16,64,128]{3,2,1,0:T(8,128)(2,1)} %copy-done.15), calls=%async_computation.6 | async-start | bytes 2097152 | tf_op jit(solution)/shard_map/all_to_all | solution.py:503
  202.5 1.9 collective-permute-start.8
  204.4 2.4 collective-permute-start.9
  206.9 1.2 collective-permute-done.9.own1p
  208.0 5.2 %shard_map.146 = (f32[224,2048]{1,0:T(8,128)S(1)}, f32[224,2048]{1,0:T(8,128)S(1)}, f32[8,128]{1,0:T(8,128)S(1)}) custom-call(bf16[4,16,128,128]{3,2,1,0:T(8,128)(2,1)S(1)} %all-to-all-done.1.refs_0_.refs_1_.came0, bf16[4,16,128,128]{3,2,1,0:T(8,128)(2,1)} %collective-permute-done.6.came0p, bf16[4,16,64,128]{3,2,1,0:T(8,128)(2,1)S(1)} %all_to_all.45.refs_0_.came1, ...), custom_call_target="tpu_custom_call" | custom-call | tf_op jit(solution)/shard_map/pallas_call | solution.py:31
  213.2 1.2 copy-done.11
  214.5 1.2 copy-done.13
  215.7 2.0 all-to-all-done.6.back
  217.8 2.3 shard_map.147
  220.1 7.9 %all-to-all-start.7 = ((bf16[16,80,128]{2,1,0:T(8,128)(2,1)}), bf16[16,80,128]{2,1,0:T(8,128)(2,1)S(1)}, u32[]{:S(2)}, u32[]{:S(2)}) async-start(bf16[16,80,128]{2,1,0:T(8,128)(2,1)} %shard_map.147), calls=%async_computation.7 | async-start | bytes 655360 | tf_op jit(solution)/shard_map/all_to_all | solution.py:507
  228.2 3.1 %collective-permute-start.3 = (bf16[2,32,64]{2,1,0:T(8,128)(2,1)S(1)}, bf16[2,32,64]{2,1,0:T(8,128)(2,1)S(1)}, u32[]{:S(2)}, u32[]{:S(2)}) collective-permute-start(bf16[2,32,64]{2,1,0:T(8,128)(2,1)S(1)} %get-tuple-element.53), channel_id=1, source_target_pairs={{0,4},{4,0},{1,5},{5,1},{2,6},{6,2},{3,7},{7,3},{8,12},{12,8},{9,1... | collective-permute-start | bytes 24584 | tf_op jit(solution)/shard_map/ppermute | solution.py:429
  231.2 0.8 collective-permute-done.3
  232.1 11.1 %all-to-all-done.7.pieces = bf16[16,80,128]{2,1,0:T(8,128)(2,1)S(1)} async-done(((bf16[16,80,128]{2,1,0:T(8,128)(2,1)}), bf16[16,80,128]{2,1,0:T(8,128)(2,1)S(1)}, u32[]{:S(2)}, u32[]{:S(2)}) %all-to-all-start.7) | async-done | bytes 327712 | tf_op jit(solution)/shard_map/all_to_all | solution.py:507
  243.1 0.7 shard_map.148
  243.9 8.5 %collective-permute-start.10 = (bf16[2,32,64]{2,1,0:T(8,128)(2,1)S(1)}, bf16[2,32,64]{2,1,0:T(8,128)(2,1)S(1)}, u32[]{:S(2)}, u32[]{:S(2)}) collective-permute-start(bf16[2,32,64]{2,1,0:T(8,128)(2,1)S(1)} %get-tuple-element.55), channel_id=1, source_target_pairs={{0,4},{4,0},{1,5},{5,1},{2,6},{6,2},{3,7},{7,3},{8,12},{12,8},{9,1... | collective-permute-start | bytes 24584 | tf_op jit(solution)/shard_map/ppermute | solution.py:429
  252.4 5.4 %all-to-all-start.8 = ((f32[32,8,128]{2,1,0:T(8,128)}), f32[32,8,128]{2,1,0:T(8,128)S(1)}, u32[]{:S(2)}, u32[]{:S(2)}) async-start(f32[32,8,128]{2,1,0:T(8,128)} %get-tuple-element.47), calls=%async_computation.8 | async-start | bytes 262144 | tf_op jit(solution)/shard_map/all_to_all | solution.py:511
  259.2 6.4 %all-to-all-done.8.refs_0_ = f32[32,8,128]{2,1,0:T(8,128)S(1)} async-done(((f32[32,8,128]{2,1,0:T(8,128)}), f32[32,8,128]{2,1,0:T(8,128)S(1)}, u32[]{:S(2)}, u32[]{:S(2)}) %all-to-all-start.8) | async-done | bytes 131104 | tf_op jit(solution)/shard_map/all_to_all | solution.py:511
  265.5 1.5 copy-done.14
  267.0 1.8 shard_map.149
  (65 shorter events, 4.1 us)
Async XLA Ops:
  0.6 0.8 copy-start.17
  1.4 0.7 copy-start.18
  2.1 0.7 copy-start.19
  2.8 0.7 copy-start.20
  3.6 0.7 copy-start.21
  4.3 9.6 %collective-permute-start = (bf16[6,32,64]{2,1,0:T(8,128)(2,1)S(1)}, bf16[6,32,64]{2,1,0:T(8,128)(2,1)S(1)}, u32[]{:S(2)}, u32[]{:S(2)}) collective-permute-start(bf16[6,32,64]{2,1,0:T(8,128)(2,1)S(1)} %get-tuple-element.29), channel_id=1, source_target_pairs={{0,4},{4,0},{1,5},{5,1},{2,6},{6,2},{3,7},{7,3},{8,12},{12,8},{9,1... | collective-permute-start | bytes 73736 | tf_op jit(solution)/shard_map/ppermute | solution.py:429
  14.9 32.3 %all-to-all-start = ((bf16[16,128,128]{2,1,0:T(8,128)(2,1)}), bf16[16,128,128]{2,1,0:T(8,128)(2,1)S(1)}, u32[]{:S(2)}, u32[]{:S(2)}) async-start(bf16[16,128,128]{2,1,0:T(8,128)(2,1)} %get-tuple-element.31), calls=%async_computation | async-start | bytes 1048576 | tf_op jit(solution)/shard_map/all_to_all | solution.py:484
  47.7 1.4 copy-start
  49.0 4.3 %copy-start.1 = (bf16[1,1,224,2048]{3,2,1,0:T(8,128)(2,1)S(1)}, bf16[1,1,224,2048]{3,2,1,0:T(8,128)(2,1)}, u32[]{:S(2)}) copy-start(bf16[1,1,224,2048]{3,2,1,0:T(8,128)(2,1)} %param.20) | copy-start | bytes 2752516
  49.0 23.1 %all-to-all-start.1 = ((bf16[4,16,128,128]{3,2,1,0:T(8,128)(2,1)}), bf16[4,16,128,128]{3,2,1,0:T(8,128)(2,1)S(1)}, u32[]{:S(2)}, u32[]{:S(2)}) async-start(bf16[4,16,128,128]{3,2,1,0:T(8,128)(2,1)} %copy-done), calls=%async_computation.1 | async-start | bytes 4194304 | tf_op jit(solution)/shard_map/all_to_all | solution.py:485
  53.4 11.4 %collective-permute-start.1 = (bf16[224,2048]{1,0:T(8,128)(2,1)S(1)}, bf16[224,2048]{1,0:T(8,128)(2,1)S(1)}, u32[]{:S(2)}, u32[]{:S(2)}) collective-permute-start(bf16[224,2048]{1,0:T(8,128)(2,1)S(1)} %bitcast.36), channel_id=1, source_target_pairs={{0,4},{4,0},{1,5},{5,1},{2,6},{6,2},{3,7},{7,3},{8,12},{12,8},{9,1... | collective-permute-start | bytes 2752520 | tf_op jit(solution)/shard_map/ppermute | solution.py:429
  62.6 4.6 %collective-permute-start.2 = (bf16[224,2048]{1,0:T(8,128)(2,1)}, bf16[224,2048]{1,0:T(8,128)(2,1)S(1)}, u32[]{:S(2)}, u32[]{:S(2)}) collective-permute-start(bf16[224,2048]{1,0:T(8,128)(2,1)} %bitcast.39), channel_id=1, source_target_pairs={{0,4},{4,0},{1,5},{5,1},{2,6},{6,2},{3,7},{7,3},{8,12},{12,8},{9,1... | collective-permute-start | bytes 2752520 | tf_op jit(solution)/shard_map/ppermute | solution.py:429
  64.7 0.9 copy-start.5
  67.2 0.9 copy-start.8
  72.1 1.2 copy-start.3
  73.3 1.2 copy-start.6
  74.5 1.2 copy-start.9
  80.5 1.0 copy-start.16
  81.5 13.2 %all-to-all-start.2 = ((bf16[4,16,64,128]{3,2,1,0:T(8,128)(2,1)}), bf16[4,16,64,128]{3,2,1,0:T(8,128)(2,1)S(1)}, u32[]{:S(2)}, u32[]{:S(2)}) async-start(bf16[4,16,64,128]{3,2,1,0:T(8,128)(2,1)} %copy-done.16), calls=%async_computation.2 | async-start | bytes 2097152 | tf_op jit(solution)/shard_map/all_to_all | solution.py:489
  95.7 36.3 %all-to-all-start.3 = ((bf16[16,64,128]{2,1,0:T(8,128)(2,1)}), bf16[16,64,128]{2,1,0:T(8,128)(2,1)S(1)}, u32[]{:S(2)}, u32[]{:S(2)}) async-start(bf16[16,64,128]{2,1,0:T(8,128)(2,1)} %shard_map.142), calls=%async_computation.3 | async-start | bytes 524288 | tf_op jit(solution)/shard_map/all_to_all | solution.py:490
  132.1 32.8 %copy-start.23 = (bf16[64,128]{1,0:T(8,128)(2,1)}, bf16[64,128]{1,0:T(8,128)(2,1)S(1)}, u32[]{:S(2)}) copy-start(bf16[64,128]{1,0:T(8,128)(2,1)S(1)} %add_convert_fusion) | copy-start | bytes 49156
  132.1 4.5 %collective-permute-start.4 = (bf16[32,128]{1,0:T(8,128)(2,1)S(1)}, bf16[32,128]{1,0:T(8,128)(2,1)S(1)}, u32[]{:S(2)}, u32[]{:S(2)}) collective-permute-start(bf16[32,128]{1,0:T(8,128)(2,1)S(1)} %get-tuple-element.65), channel_id=1, source_target_pairs={{0,128},{128,256},{256,384},{1,129},{129,257},{257,385},{2,130},{1... | collective-permute-start | bytes 24584 | tf_op jit(solution)/shard_map/ppermute | solution.py:434
  135.2 4.4 %collective-permute-start.5 = (bf16[32,128]{1,0:T(8,128)(2,1)S(1)}, bf16[32,128]{1,0:T(8,128)(2,1)S(1)}, u32[]{:S(2)}, u32[]{:S(2)}) collective-permute-start(bf16[32,128]{1,0:T(8,128)(2,1)S(1)} %get-tuple-element.64), channel_id=1, source_target_pairs={{128,0},{256,128},{384,256},{129,1},{257,129},{385,257},{130,2},{2... | collective-permute-start | bytes 24584 | tf_op jit(solution)/shard_map/ppermute | solution.py:434
  141.1 23.5 %all-to-all-start.4 = ((bf16[16,64,128]{2,1,0:T(8,128)(2,1)}), bf16[16,64,128]{2,1,0:T(8,128)(2,1)S(1)}, u32[]{:S(2)}, u32[]{:S(2)}) async-start(bf16[16,64,128]{2,1,0:T(8,128)(2,1)} %get-tuple-element.35), calls=%async_computation.4 | async-start | bytes 524288 | tf_op jit(solution)/shard_map/all_to_all | solution.py:498
  151.8 55.1 %collective-permute-start.6 = (bf16[4,16,128,128]{3,2,1,0:T(8,128)(2,1)S(1)}, bf16[4,16,128,128]{3,2,1,0:T(8,128)(2,1)}, u32[]{:S(2)}, u32[]{:S(2)}) collective-permute-start(bf16[4,16,128,128]{3,2,1,0:T(8,128)(2,1)S(1)} %all-to-all-done.1.refs_0_.refs_1_.came0), channel_id=1, source_target_pairs={{0,4},{4,0},{1,5},{5,1},{2,6},{6,2},{3,7},{7,3},{8,12},{12,8},{9,1... | collective-permute-start | bytes 6291464 | tf_op jit(solution)/shard_map/ppermute | solution.py:429
  177.0 1.2 copy-start.2
  178.2 1.2 copy-start.4
  179.4 1.2 copy-start.7
  180.5 1.2 copy-start.10
  186.6 1.0 copy-start.15
  187.7 0.7 copy-start.22
  188.3 19.7 %collective-permute-start.7 = (bf16[4,16,64,128]{3,2,1,0:T(8,128)(2,1)S(1)}, bf16[4,16,64,128]{3,2,1,0:T(8,128)(2,1)}, u32[]{:S(2)}, u32[]{:S(2)}) collective-permute-start(bf16[4,16,64,128]{3,2,1,0:T(8,128)(2,1)S(1)} %all_to_all.45.refs_0_.came1), channel_id=1, source_target_pairs={{0,4},{4,0},{1,5},{5,1},{2,6},{6,2},{3,7},{7,3},{8,12},{12,8},{9,1... | collective-permute-start | bytes 3145736 | tf_op jit(solution)/shard_map/ppermute | solution.py:429
  198.2 19.5 %all-to-all-start.6 = ((bf16[4,16,64,128]{3,2,1,0:T(8,128)(2,1)}), bf16[4,16,64,128]{3,2,1,0:T(8,128)(2,1)}, u32[]{:S(2)}, u32[]{:S(2)}) async-start(bf16[4,16,64,128]{3,2,1,0:T(8,128)(2,1)} %copy-done.15), calls=%async_computation.6 | async-start | bytes 2097152 | tf_op jit(solution)/shard_map/all_to_all | solution.py:503
  202.5 4.3 %collective-permute-start.8 = (bf16[2,128,224]{2,1,0:T(8,128)(2,1)S(1)}, bf16[2,128,224]{2,1,0:T(8,128)(2,1)S(1)}, u32[]{:S(2)}, u32[]{:S(2)}) collective-permute-start(bf16[2,128,224]{2,1,0:T(8,128)(2,1)S(1)} %get-tuple-element.41), channel_id=1, source_target_pairs={{0,4},{4,0},{1,5},{5,1},{2,6},{6,2},{3,7},{7,3},{8,12},{12,8},{9,1... | collective-permute-start | bytes 344072 | tf_op jit(solution)/shard_map/ppermute | solution.py:429
  204.4 3.6 %collective-permute-start.9 = (bf16[2,128,224]{2,1,0:T(8,128)(2,1)}, bf16[2,128,224]{2,1,0:T(8,128)(2,1)S(1)}, u32[]{:S(2)}, u32[]{:S(2)}) collective-permute-start(bf16[2,128,224]{2,1,0:T(8,128)(2,1)} %copy-done.22), channel_id=1, source_target_pairs={{0,4},{4,0},{1,5},{5,1},{2,6},{6,2},{3,7},{7,3},{8,12},{12,8},{9,1... | collective-permute-start | bytes 344072 | tf_op jit(solution)/shard_map/ppermute | solution.py:429
  208.0 9.7 %copy-start.25 = (f32[4,32]{1,0:T(4,128)S(1)}, f32[4,32]{1,0:T(4,128)}, u32[]{:S(2)}) copy-start(f32[4,32]{1,0:T(4,128)} %get-tuple-element.66) | copy-start | bytes 1540
  213.2 1.3 copy-start.11
  214.5 1.2 copy-start.13
  215.7 12.3 %copy-start.24 = (bf16[64,128]{1,0:T(8,128)(2,1)S(1)}, bf16[64,128]{1,0:T(8,128)(2,1)}, u32[]{:S(2)}) copy-start(bf16[64,128]{1,0:T(8,128)(2,1)} %copy-done.23) | copy-start | bytes 49156
  217.7 47.8 %copy-start.12 = (f32[224,2048]{1,0:T(8,128)S(1)}, f32[224,2048]{1,0:T(8,128)}, u32[]{:S(2)}) copy-start(f32[224,2048]{1,0:T(8,128)} %copy-done.11) | copy-start | bytes 5505028
  220.1 23.0 %all-to-all-start.7 = ((bf16[16,80,128]{2,1,0:T(8,128)(2,1)}), bf16[16,80,128]{2,1,0:T(8,128)(2,1)S(1)}, u32[]{:S(2)}, u32[]{:S(2)}) async-start(bf16[16,80,128]{2,1,0:T(8,128)(2,1)} %shard_map.147), calls=%async_computation.7 | async-start | bytes 655360 | tf_op jit(solution)/shard_map/all_to_all | solution.py:507
  228.2 3.9 %collective-permute-start.3 = (bf16[2,32,64]{2,1,0:T(8,128)(2,1)S(1)}, bf16[2,32,64]{2,1,0:T(8,128)(2,1)S(1)}, u32[]{:S(2)}, u32[]{:S(2)}) collective-permute-start(bf16[2,32,64]{2,1,0:T(8,128)(2,1)S(1)} %get-tuple-element.53), channel_id=1, source_target_pairs={{0,4},{4,0},{1,5},{5,1},{2,6},{6,2},{3,7},{7,3},{8,12},{12,8},{9,1... | collective-permute-start | bytes 24584 | tf_op jit(solution)/shard_map/ppermute | solution.py:429
  243.9 13.9 %collective-permute-start.10 = (bf16[2,32,64]{2,1,0:T(8,128)(2,1)S(1)}, bf16[2,32,64]{2,1,0:T(8,128)(2,1)S(1)}, u32[]{:S(2)}, u32[]{:S(2)}) collective-permute-start(bf16[2,32,64]{2,1,0:T(8,128)(2,1)S(1)} %get-tuple-element.55), channel_id=1, source_target_pairs={{0,4},{4,0},{1,5},{5,1},{2,6},{6,2},{3,7},{7,3},{8,12},{12,8},{9,1... | collective-permute-start | bytes 24584 | tf_op jit(solution)/shard_map/ppermute | solution.py:429
  252.4 13.1 %all-to-all-start.8 = ((f32[32,8,128]{2,1,0:T(8,128)}), f32[32,8,128]{2,1,0:T(8,128)S(1)}, u32[]{:S(2)}, u32[]{:S(2)}) async-start(f32[32,8,128]{2,1,0:T(8,128)} %get-tuple-element.47), calls=%async_computation.8 | async-start | bytes 262144 | tf_op jit(solution)/shard_map/all_to_all | solution.py:511
  265.5 1.5 copy-start.14

commit v2 on v1

--- a/solution.py
+++ b/solution.py
@@ -30,12 +30,15 @@
 def call(body, outs, args, scratch=(), limit=24):
     return pl.pallas_call(
         body,
-        out_shape=tuple(jax.ShapeDtypeStruct(shape, dtype) for shape, dtype, _ in outs),
+        out_shape=tuple(
+            pltpu.HBM(shape, dtype) if space == HBM else jax.ShapeDtypeStruct(shape, dtype)
+            for shape, dtype, space in outs
+        ),
         in_specs=[pl.BlockSpec(memory_space=space) for _, space in args],
         out_specs=tuple(pl.BlockSpec(memory_space=space) for _, _, space in outs),
         scratch_shapes=list(scratch),
         compiler_params=pltpu.CompilerParams(vmem_limit_bytes=limit * 1024 * 1024),
-    )(*(array for array, _ in args))
+    )(*(pltpu.with_memory_space_constraint(a, HBM) if space == HBM else a for a, space in args))
 
 
 def sems(number):
@@ -47,11 +50,18 @@
 
 
 def pack_body(core, *refs):
-    inputs, (send, keep) = refs[:-2], refs[-2:]
+    count = (len(refs) - 3) // 2
+    inputs, (send, keep), held, arrived = refs[:count], refs[count : count + 2], refs[count + 2 : -1], refs[-1]
+    copies = [
+        pltpu.make_async_copy(ref, to, arrived.at[n]) for n, (ref, to) in enumerate(zip(inputs, held))
+    ]
+    for c in copies:
+        c.start()
     mine = pl.multiple_of(core[0] * ROWS, ROWS)
     others = pl.multiple_of((1 - core[0]) * ROWS, ROWS)
     at = 0
-    for ref in inputs:
+    for c, ref in zip(copies, held):
+        c.wait()
         for n in range(ref.shape[0]):
             keep[at] = ref[n, pl.ds(mine, ROWS), :]
             send[at] = ref[n, pl.ds(others, ROWS), :]
@@ -64,7 +74,8 @@
     return call(
         pack_body,
         ((shape, BF, VMEM), (shape, BF, VMEM)),
-        ((core, SMEM), *((a, VMEM) for a in arrays)),
+        ((core, SMEM), *((a, HBM) for a in arrays)),
+        scratch=(*(pltpu.VMEM(a.shape, BF) for a in arrays), sems(len(arrays))),
     )
 
 
@@ -429,6 +440,10 @@
     return lax.ppermute(value, "core", [(0, 1), (1, 0)])
 
 
+def exchanged(value, axis):
+    return lax.all_to_all(value, axis, 0, 0, tiled=True)
+
+
 def shifted(value, steps):
     count = lax.axis_size("section")
     return lax.ppermute(
@@ -481,13 +496,13 @@
     fwd_weight = gate_rows(fwd_experts[0], fwd_gates[0])
     bwd_weight = gate_rows(bwd_experts[0], bwd_gates[0])
 
-    got = lax.all_to_all(outgoing, "z", 0, 0, tiled=True)
-    came0 = lax.all_to_all(spread(got, bwd_weight[0]), "dp", 0, 0, tiled=True)
+    got = exchanged(outgoing, "z")
+    came0 = exchanged(spread(got, bwd_weight[0]), "dp")
     partial, own0, other0 = layer(came0, None, None, weights)
     came0, partial = lax.optimization_barrier((came0, partial))
     came0p, own0p = swapped(came0), swapped(other0)
-    back = lax.all_to_all(partial, "dp", 0, 0, tiled=True)
-    pieces = lax.all_to_all(combine(back, fwd_weight[0]), "z", 0, 0, tiled=True)
+    back = exchanged(partial, "dp")
+    pieces = exchanged(combine(back, fwd_weight[0]), "z")
     base = first[0 : 2 * ROWS]
     result0 = (base.astype(F32) + jnp.sum(pieces.astype(F32), axis=0)).astype(BF)
 
@@ -495,20 +510,19 @@
     leaving = shifted(result0[ROWS : 2 * ROWS], -1)
     outgoing, second = following(place, arriving, leaving, fresh)
 
-    got = lax.all_to_all(outgoing, "z", 0, 0, tiled=True)
-    came1 = lax.all_to_all(spread(got, bwd_weight[1]), "dp", 0, 0, tiled=True)
+    got = exchanged(outgoing, "z")
+    came1 = exchanged(spread(got, bwd_weight[1]), "dp")
     partial, own1, other1 = layer(came1, came0, 3 * ROWS, weights)
     came1, partial = lax.optimization_barrier((came1, partial))
     came1p, own1p = swapped(came1), swapped(other1)
-    back = lax.all_to_all(partial, "dp", 0, 0, tiled=True)
+    back = exchanged(partial, "dp")
     gate_total, down_total, squares = grads(
         (came0, came0p, came1, came1p), (own0, own0p, own1, own1p)
     )
-    pieces = lax.all_to_all(combine(back, fwd_weight[1], squares), "z", 0, 0, tiled=True)
-
-    plane = ("section", "dp", "core")
+    pieces = exchanged(combine(back, fwd_weight[1], squares), "z")
+
     result1, tiles = closed(pieces, second, 32)
-    tiles = lax.all_to_all(tiles, plane, 0, 0, tiled=True)
+    tiles = exchanged(tiles, ("section", "dp", "core"))
     clip_limit = 0.25 * math.sqrt(2.0 * section_count * EXPERTS * FF * D)
     gate_grad, down_grad = clipped(clip_limit, tiles, gate_total, down_total)
 

time: 271 us -> 260 us (0.959)
  local copies, waits for them, and re-layouts: 24.5 us -> 4.3 us
  Pallas kernels: 23.7 us -> 29.6 us
  waiting for transfers between devices: 81.7 us -> 85.7 us
    unnamed x52 -> x16, local copies, waits for them, and re-layouts: 21.8 us -> 1.6 us
    pallas_call x12, Pallas kernels: 23.7 us -> 29.6 us  [call(): pl.pallas_call(body, out_shape=tuple((pltpu.HBM(shape, dtype) if space ==...]
    all_to_all x8, waiting for transfers between devices: 74.1 us -> 78 us  [exchanged(): return lax.all_to_all(value, axis, 0, 0, tiled=True)]
  transfers between devices with their start and end apart: 19 -> 19, of which waited for: 14 -> 14; matrix products, arithmetic and copies ran while one was open for 1% -> 1% of each run, Pallas kernels for 4% -> 5%
where the time goes in v2:
time: 260 us; the launch traced here: 259 us
  starting transfers between devices  124 us (48%)
  waiting for transfers between devices  85.7 us (33%)
  Pallas kernels  29.6 us (11%)
  blocking collectives  13.2 us (5%)
  local copies, waits for them, and re-layouts  4.3 us (2%)
    all_to_all x8, waiting for transfers between devices, exchanged(): return lax.all_to_all(value, axis, 0, 0, tiled=True)  78 us
    all_to_all x8, starting transfers between devices, exchanged(): return lax.all_to_all(value, axis, 0, 0, tiled=True)  68.7 us
    ppermute x9, starting transfers between devices, swapped(): return lax.ppermute(value, 'core', [(0, 1), (1, 0)])  50.7 us
    pallas_call x12, Pallas kernels, call(): pl.pallas_call(body, out_shape=tuple((pltpu.HBM(shape, dtype) if space ==...  29.6 us
    all_to_all x1, blocking collectives, exchanged(): return lax.all_to_all(value, axis, 0, 0, tiled=True)  13.2 us
  transfers between devices with their start and end apart: 19, of which 14 were waited for; matrix products, arithmetic and copies ran while one was open for 1% of the time, Pallas kernels for 5%

profile of v2, /device:TPU:1, one launch (start us, length us, event | category | flops | bytes accessed | tf_op | source)
XLA Modules:
  0.0 259.2 jit_solution(7870751732157671450)
XLA Ops:
  0.6 0.9 shard_map.138
  1.5 8.7 %collective-permute-start = (bf16[6,32,64]{2,1,0:T(8,128)(2,1)S(1)}, bf16[6,32,64]{2,1,0:T(8,128)(2,1)S(1)}, u32[]{:S(2)}, u32[]{:S(2)}) collective-permute-start(bf16[6,32,64]{2,1,0:T(8,128)(2,1)S(1)} %get-tuple-element.29), channel_id=1, source_target_pairs={{0,4},{4,0},{1,5},{5,1},{2,6},{6,2},{3,7},{7,3},{8,12},{12,8},{9,1... | collective-permute-start | bytes 73736 | tf_op jit(solution)/shard_map/ppermute | solution.py:440
  10.3 0.9 collective-permute-done.got
  11.1 1.0 shard_map.139
  12.1 9.6 %all-to-all-start = ((bf16[16,128,128]{2,1,0:T(8,128)(2,1)}), bf16[16,128,128]{2,1,0:T(8,128)(2,1)S(1)}, u32[]{:S(2)}, u32[]{:S(2)}) async-start(bf16[16,128,128]{2,1,0:T(8,128)(2,1)} %get-tuple-element.31), calls=%async_computation | async-start | bytes 1048576 | tf_op jit(solution)/shard_map/all_to_all | solution.py:444
  21.7 0.8 dynamic-slice_bitcast_fusion
  22.5 0.8 dynamic-slice_bitcast_fusion.1
  23.3 21.2 %all-to-all-done.got = bf16[16,128,128]{2,1,0:T(8,128)(2,1)S(1)} async-done(((bf16[16,128,128]{2,1,0:T(8,128)(2,1)}), bf16[16,128,128]{2,1,0:T(8,128)(2,1)S(1)}, u32[]{:S(2)}, u32[]{:S(2)}) %all-to-all-start) | async-done | bytes 524320 | tf_op jit(solution)/shard_map/all_to_all | solution.py:444
  44.4 0.1 broadcast_in_dim.72.weight
  44.5 1.4 shard_map.140
  46.0 0.0 copy-start.3
  46.0 4.3 %all-to-all-start.1 = ((bf16[4,16,128,128]{3,2,1,0:T(8,128)(2,1)}), bf16[4,16,128,128]{3,2,1,0:T(8,128)(2,1)S(1)}, u32[]{:S(2)}, u32[]{:S(2)}) async-start(bf16[4,16,128,128]{3,2,1,0:T(8,128)(2,1)} %shard_map.140), calls=%async_computation.1 | async-start | bytes 4194304 | tf_op jit(solution)/shard_map/all_to_all | solution.py:444
  50.3 9.3 %collective-permute-start.1 = (bf16[224,2048]{1,0:T(8,128)(2,1)S(1)}, bf16[224,2048]{1,0:T(8,128)(2,1)S(1)}, u32[]{:S(2)}, u32[]{:S(2)}) collective-permute-start(bf16[224,2048]{1,0:T(8,128)(2,1)S(1)} %bitcast.38), channel_id=1, source_target_pairs={{0,4},{4,0},{1,5},{5,1},{2,6},{6,2},{3,7},{7,3},{8,12},{12,8},{9,1... | collective-permute-start | bytes 2752520 | tf_op jit(solution)/shard_map/ppermute | solution.py:440
  59.6 1.9 collective-permute-start.2
  61.5 0.1 collective-permute-done.1.refs_2_.refs_3_
  61.7 0.9 copy-done.4
  62.6 1.7 collective-permute-done.2.refs_4_.refs_5_
  64.3 4.7 %all-to-all-done.1.refs_0_.refs_1_.came0 = bf16[4,16,128,128]{3,2,1,0:T(8,128)(2,1)S(1)} async-done(((bf16[4,16,128,128]{3,2,1,0:T(8,128)(2,1)}), bf16[4,16,128,128]{3,2,1,0:T(8,128)(2,1)S(1)}, u32[]{:S(2)}, u32[]{:S(2)}) %all-to-all-start.1) | async-done | bytes 2097184 | tf_op jit(solution)/shard_map/all_to_all | solution.py:444
  69.0 6.2 %shard_map.141 = (bf16[4,16,64,128]{3,2,1,0:T(8,128)(2,1)}, bf16[2,128,224]{2,1,0:T(8,128)(2,1)S(1)}, bf16[2,128,224]{2,1,0:T(8,128)(2,1)S(1)}) custom-call(bf16[4,16,128,128]{3,2,1,0:T(8,128)(2,1)S(1)} %all-to-all-done.1.refs_0_.refs_1_.came0, bf16[224,2048]{1,0:T(8,128)(2,1)} %bitcast.36, bf16[224,2048]{1,0:T(8,128)(2,1)} %copy-done.4, ...), custom_call_target="tpu_custom_call" | custom-call | tf_op jit(solution)/shard_map/pallas_call | solution.py:31
  75.3 3.5 %all-to-all-start.2 = ((bf16[4,16,64,128]{3,2,1,0:T(8,128)(2,1)}), bf16[4,16,64,128]{3,2,1,0:T(8,128)(2,1)S(1)}, u32[]{:S(2)}, u32[]{:S(2)}) async-start(bf16[4,16,64,128]{3,2,1,0:T(8,128)(2,1)} %get-tuple-element.33), calls=%async_computation.2 | async-start | bytes 2097152 | tf_op jit(solution)/shard_map/all_to_all | solution.py:444
  78.8 0.6 slice_bitcast_fusion
  79.4 9.1 %all-to-all-done.2.back = bf16[4,16,64,128]{3,2,1,0:T(8,128)(2,1)S(1)} async-done(((bf16[4,16,64,128]{3,2,1,0:T(8,128)(2,1)}), bf16[4,16,64,128]{3,2,1,0:T(8,128)(2,1)S(1)}, u32[]{:S(2)}, u32[]{:S(2)}) %all-to-all-start.2) | async-done | bytes 1048608 | tf_op jit(solution)/shard_map/all_to_all | solution.py:444
  88.5 0.1 broadcast_in_dim.76.weight
  88.6 0.9 shard_map.142
  89.5 23.6 %all-to-all-start.3 = ((bf16[16,64,128]{2,1,0:T(8,128)(2,1)}), bf16[16,64,128]{2,1,0:T(8,128)(2,1)S(1)}, u32[]{:S(2)}, u32[]{:S(2)}) async-start(bf16[16,64,128]{2,1,0:T(8,128)(2,1)} %shard_map.142), calls=%async_computation.3 | async-start | bytes 524288 | tf_op jit(solution)/shard_map/all_to_all | solution.py:444
  113.1 12.7 %all-to-all-done.3 = bf16[16,64,128]{2,1,0:T(8,128)(2,1)S(1)} async-done(((bf16[16,64,128]{2,1,0:T(8,128)(2,1)}), bf16[16,64,128]{2,1,0:T(8,128)(2,1)S(1)}, u32[]{:S(2)}, u32[]{:S(2)}) %all-to-all-start.3) | async-done | bytes 262176 | tf_op jit(solution)/shard_map/all_to_all | solution.py:444
  125.8 0.0 copy-start.5
  125.9 3.1 %collective-permute-start.4 = (bf16[32,128]{1,0:T(8,128)(2,1)S(1)}, bf16[32,128]{1,0:T(8,128)(2,1)S(1)}, u32[]{:S(2)}, u32[]{:S(2)}) collective-permute-start(bf16[32,128]{1,0:T(8,128)(2,1)S(1)} %get-tuple-element.65), channel_id=1, source_target_pairs={{0,128},{128,256},{256,384},{1,129},{129,257},{257,385},{2,130},{1... | collective-permute-start | bytes 24584 | tf_op jit(solution)/shard_map/ppermute | solution.py:449
  129.0 1.3 collective-permute-start.5
  130.3 0.1 pad_add_fusion.place
  130.4 3.0 %collective-permute-done.5.leaving = bf16[32,128]{1,0:T(8,128)(2,1)S(1)} collective-permute-done((bf16[32,128]{1,0:T(8,128)(2,1)S(1)}, bf16[32,128]{1,0:T(8,128)(2,1)S(1)}, u32[]{:S(2)}, u32[]{:S(2)}) %collective-permute-start.5) | collective-permute-done | bytes 8224 | tf_op jit(solution)/shard_map/ppermute | solution.py:449
  133.4 1.4 shard_map.143
  134.8 10.7 %all-to-all-start.4 = ((bf16[16,64,128]{2,1,0:T(8,128)(2,1)}), bf16[16,64,128]{2,1,0:T(8,128)(2,1)S(1)}, u32[]{:S(2)}, u32[]{:S(2)}) async-start(bf16[16,64,128]{2,1,0:T(8,128)(2,1)} %get-tuple-element.35), calls=%async_computation.4 | async-start | bytes 524288 | tf_op jit(solution)/shard_map/all_to_all | solution.py:444
  145.5 5.0 %collective-permute-start.6 = (bf16[4,16,128,128]{3,2,1,0:T(8,128)(2,1)S(1)}, bf16[4,16,128,128]{3,2,1,0:T(8,128)(2,1)}, u32[]{:S(2)}, u32[]{:S(2)}) collective-permute-start(bf16[4,16,128,128]{3,2,1,0:T(8,128)(2,1)S(1)} %all-to-all-done.1.refs_0_.refs_1_.came0), channel_id=1, source_target_pairs={{0,4},{4,0},{1,5},{5,1},{2,6},{6,2},{3,7},{7,3},{8,12},{12,8},{9,1... | collective-permute-start | bytes 6291464 | tf_op jit(solution)/shard_map/ppermute | solution.py:440
  150.5 7.7 %all-to-all-done.4.got = bf16[16,64,128]{2,1,0:T(8,128)(2,1)S(1)} async-done(((bf16[16,64,128]{2,1,0:T(8,128)(2,1)}), bf16[16,64,128]{2,1,0:T(8,128)(2,1)S(1)}, u32[]{:S(2)}, u32[]{:S(2)}) %all-to-all-start.4) | async-done | bytes 262176 | tf_op jit(solution)/shard_map/all_to_all | solution.py:444
  158.2 0.1 broadcast_in_dim.78.weight
  158.3 1.1 shard_map.144
  159.4 13.2 %all_to_all.45.refs_0_.came1 = bf16[4,16,64,128]{3,2,1,0:T(8,128)(2,1)S(1)} all-to-all(bf16[4,16,64,128]{3,2,1,0:T(8,128)(2,1)} %shard_map.144), channel_id=1, replica_groups=mesh['section'=4,'z'=16,'core'=2,'dp'=4] {'dp'}, dimensions={0} | all-to-all | bytes 2097152 | tf_op jit(solution)/shard_map/all_to_all | solution.py:444
  172.7 6.2 %shard_map.145 = (bf16[4,16,64,128]{3,2,1,0:T(8,128)(2,1)}, bf16[2,128,224]{2,1,0:T(8,128)(2,1)S(1)}, bf16[2,128,224]{2,1,0:T(8,128)(2,1)S(1)}) custom-call(bf16[4,16,64,128]{3,2,1,0:T(8,128)(2,1)S(1)} %all_to_all.45.refs_0_.came1, bf16[4,16,128,128]{3,2,1,0:T(8,128)(2,1)} %copy-done, bf16[224,2048]{1,0:T(8,128)(2,1)} %bitcast.37, ...), custom_call_target="tpu_custom_call" | custom-call | tf_op jit(solution)/shard_map/pallas_call | solution.py:31
  178.9 0.6 copy-done.2
  179.5 9.9 %collective-permute-start.7 = (bf16[4,16,64,128]{3,2,1,0:T(8,128)(2,1)S(1)}, bf16[4,16,64,128]{3,2,1,0:T(8,128)(2,1)}, u32[]{:S(2)}, u32[]{:S(2)}) collective-permute-start(bf16[4,16,64,128]{3,2,1,0:T(8,128)(2,1)S(1)} %all_to_all.45.refs_0_.came1), channel_id=1, source_target_pairs={{0,4},{4,0},{1,5},{5,1},{2,6},{6,2},{3,7},{7,3},{8,12},{12,8},{9,1... | collective-permute-start | bytes 3145736 | tf_op jit(solution)/shard_map/ppermute | solution.py:440
  189.4 4.3 %all-to-all-start.6 = ((bf16[4,16,64,128]{3,2,1,0:T(8,128)(2,1)}), bf16[4,16,64,128]{3,2,1,0:T(8,128)(2,1)}, u32[]{:S(2)}, u32[]{:S(2)}) async-start(bf16[4,16,64,128]{3,2,1,0:T(8,128)(2,1)} %get-tuple-element.38), calls=%async_computation.6 | async-start | bytes 2097152 | tf_op jit(solution)/shard_map/all_to_all | solution.py:444
  193.7 1.9 collective-permute-start.8
  195.6 2.4 collective-permute-start.9
  198.1 1.2 collective-permute-done.9.own1p
  199.2 4.6 %shard_map.146 = (f32[224,2048]{1,0:T(8,128)}, f32[224,2048]{1,0:T(8,128)}, f32[8,128]{1,0:T(8,128)S(1)}) custom-call(bf16[4,16,128,128]{3,2,1,0:T(8,128)(2,1)} %copy-done, bf16[4,16,128,128]{3,2,1,0:T(8,128)(2,1)} %collective-permute-done.6.came0p, bf16[4,16,64,128]{3,2,1,0:T(8,128)(2,1)} %copy-done.1, ...), custom_call_target="tpu_custom_call" | custom-call | tf_op jit(solution)/shard_map/pallas_call | solution.py:31
  203.8 5.1 %all-to-all-done.6.back = bf16[4,16,64,128]{3,2,1,0:T(8,128)(2,1)} async-done(((bf16[4,16,64,128]{3,2,1,0:T(8,128)(2,1)}), bf16[4,16,64,128]{3,2,1,0:T(8,128)(2,1)}, u32[]{:S(2)}, u32[]{:S(2)}) %all-to-all-start.6) | async-done | bytes 1048608 | tf_op jit(solution)/shard_map/all_to_all | solution.py:444
  208.9 0.1 broadcast_in_dim.80.weight
  209.0 2.2 shard_map.147
  211.2 7.9 %all-to-all-start.7 = ((bf16[16,80,128]{2,1,0:T(8,128)(2,1)}), bf16[16,80,128]{2,1,0:T(8,128)(2,1)S(1)}, u32[]{:S(2)}, u32[]{:S(2)}) async-start(bf16[16,80,128]{2,1,0:T(8,128)(2,1)} %shard_map.147), calls=%async_computation.7 | async-start | bytes 655360 | tf_op jit(solution)/shard_map/all_to_all | solution.py:444
  219.1 0.1 reshape.44
  219.2 0.1 fusion.2
  219.2 3.1 %collective-permute-start.3 = (bf16[2,32,64]{2,1,0:T(8,128)(2,1)S(1)}, bf16[2,32,64]{2,1,0:T(8,128)(2,1)S(1)}, u32[]{:S(2)}, u32[]{:S(2)}) collective-permute-start(bf16[2,32,64]{2,1,0:T(8,128)(2,1)S(1)} %get-tuple-element.53), channel_id=1, source_target_pairs={{0,4},{4,0},{1,5},{5,1},{2,6},{6,2},{3,7},{7,3},{8,12},{12,8},{9,1... | collective-permute-start | bytes 24584 | tf_op jit(solution)/shard_map/ppermute | solution.py:440
  222.3 0.8 collective-permute-done.3
  223.1 11.1 %all-to-all-done.7.pieces = bf16[16,80,128]{2,1,0:T(8,128)(2,1)S(1)} async-done(((bf16[16,80,128]{2,1,0:T(8,128)(2,1)}), bf16[16,80,128]{2,1,0:T(8,128)(2,1)S(1)}, u32[]{:S(2)}, u32[]{:S(2)}) %all-to-all-start.7) | async-done | bytes 327712 | tf_op jit(solution)/shard_map/all_to_all | solution.py:444
  234.2 0.7 shard_map.148
  234.9 0.1 reshape.45
  235.0 0.1 fusion.3
  235.0 8.5 %collective-permute-start.10 = (bf16[2,32,64]{2,1,0:T(8,128)(2,1)S(1)}, bf16[2,32,64]{2,1,0:T(8,128)(2,1)S(1)}, u32[]{:S(2)}, u32[]{:S(2)}) collective-permute-start(bf16[2,32,64]{2,1,0:T(8,128)(2,1)S(1)} %get-tuple-element.55), channel_id=1, source_target_pairs={{0,4},{4,0},{1,5},{5,1},{2,6},{6,2},{3,7},{7,3},{8,12},{12,8},{9,1... | collective-permute-start | bytes 24584 | tf_op jit(solution)/shard_map/ppermute | solution.py:440
  243.5 4.9 %all-to-all-start.8 = ((f32[32,8,128]{2,1,0:T(8,128)}), f32[32,8,128]{2,1,0:T(8,128)S(1)}, u32[]{:S(2)}, u32[]{:S(2)}) async-start(f32[32,8,128]{2,1,0:T(8,128)} %get-tuple-element.47), calls=%async_computation.8 | async-start | bytes 262144 | tf_op jit(solution)/shard_map/all_to_all | solution.py:444
  248.5 0.6 maximum_bitcast_fusion.1
  249.1 0.6 maximum_bitcast_fusion
  249.7 6.4 %all-to-all-done.8.refs_0_ = f32[32,8,128]{2,1,0:T(8,128)S(1)} async-done(((f32[32,8,128]{2,1,0:T(8,128)}), f32[32,8,128]{2,1,0:T(8,128)S(1)}, u32[]{:S(2)}, u32[]{:S(2)}) %all-to-all-start.8) | async-done | bytes 131104 | tf_op jit(solution)/shard_map/all_to_all | solution.py:444
  256.1 3.1 %shard_map.149 = (bf16[224,2048]{1,0:T(8,128)(2,1)}, bf16[224,2048]{1,0:T(8,128)(2,1)}) custom-call(f32[32,8,128]{2,1,0:T(8,128)S(1)} %all-to-all-done.8.refs_0_, f32[224,2048]{1,0:T(8,128)} %get-tuple-element.48.refs_1_, f32[224,2048]{1,0:T(8,128)} %get-tuple-element.49.refs_2_), custom_call_target="tpu_custom_call" | custom-call | tf_op jit(solution)/shard_map/pallas_call | solution.py:31
  (29 shorter events, 0.2 us)
Async XLA Ops:
  1.5 9.6 %collective-permute-start = (bf16[6,32,64]{2,1,0:T(8,128)(2,1)S(1)}, bf16[6,32,64]{2,1,0:T(8,128)(2,1)S(1)}, u32[]{:S(2)}, u32[]{:S(2)}) collective-permute-start(bf16[6,32,64]{2,1,0:T(8,128)(2,1)S(1)} %get-tuple-element.29), channel_id=1, source_target_pairs={{0,4},{4,0},{1,5},{5,1},{2,6},{6,2},{3,7},{7,3},{8,12},{12,8},{9,1... | collective-permute-start | bytes 73736 | tf_op jit(solution)/shard_map/ppermute | solution.py:440
  12.1 32.3 %all-to-all-start = ((bf16[16,128,128]{2,1,0:T(8,128)(2,1)}), bf16[16,128,128]{2,1,0:T(8,128)(2,1)S(1)}, u32[]{:S(2)}, u32[]{:S(2)}) async-start(bf16[16,128,128]{2,1,0:T(8,128)(2,1)} %get-tuple-element.31), calls=%async_computation | async-start | bytes 1048576 | tf_op jit(solution)/shard_map/all_to_all | solution.py:444
  46.0 4.3 %copy-start.3 = (bf16[1,1,224,2048]{3,2,1,0:T(8,128)(2,1)S(1)}, bf16[1,1,224,2048]{3,2,1,0:T(8,128)(2,1)}, u32[]{:S(2)}) copy-start(bf16[1,1,224,2048]{3,2,1,0:T(8,128)(2,1)} %param.20) | copy-start | bytes 2752516
  46.0 23.1 %all-to-all-start.1 = ((bf16[4,16,128,128]{3,2,1,0:T(8,128)(2,1)}), bf16[4,16,128,128]{3,2,1,0:T(8,128)(2,1)S(1)}, u32[]{:S(2)}, u32[]{:S(2)}) async-start(bf16[4,16,128,128]{3,2,1,0:T(8,128)(2,1)} %shard_map.140), calls=%async_computation.1 | async-start | bytes 4194304 | tf_op jit(solution)/shard_map/all_to_all | solution.py:444
  50.3 11.4 %collective-permute-start.1 = (bf16[224,2048]{1,0:T(8,128)(2,1)S(1)}, bf16[224,2048]{1,0:T(8,128)(2,1)S(1)}, u32[]{:S(2)}, u32[]{:S(2)}) collective-permute-start(bf16[224,2048]{1,0:T(8,128)(2,1)S(1)} %bitcast.38), channel_id=1, source_target_pairs={{0,4},{4,0},{1,5},{5,1},{2,6},{6,2},{3,7},{7,3},{8,12},{12,8},{9,1... | collective-permute-start | bytes 2752520 | tf_op jit(solution)/shard_map/ppermute | solution.py:440
  59.6 4.7 %collective-permute-start.2 = (bf16[224,2048]{1,0:T(8,128)(2,1)}, bf16[224,2048]{1,0:T(8,128)(2,1)}, u32[]{:S(2)}, u32[]{:S(2)}) collective-permute-start(bf16[224,2048]{1,0:T(8,128)(2,1)} %bitcast.39), channel_id=1, source_target_pairs={{0,4},{4,0},{1,5},{5,1},{2,6},{6,2},{3,7},{7,3},{8,12},{12,8},{9,1... | collective-permute-start | bytes 2752520 | tf_op jit(solution)/shard_map/ppermute | solution.py:440
  61.7 0.9 copy-start.4
  69.0 76.5 %copy-start = (bf16[4,16,128,128]{3,2,1,0:T(8,128)(2,1)}, bf16[4,16,128,128]{3,2,1,0:T(8,128)(2,1)S(1)}, u32[]{:S(2)}) copy-start(bf16[4,16,128,128]{3,2,1,0:T(8,128)(2,1)S(1)} %all-to-all-done.1.refs_0_.refs_1_.came0) | copy-start | bytes 6291460
  75.3 13.2 %all-to-all-start.2 = ((bf16[4,16,64,128]{3,2,1,0:T(8,128)(2,1)}), bf16[4,16,64,128]{3,2,1,0:T(8,128)(2,1)S(1)}, u32[]{:S(2)}, u32[]{:S(2)}) async-start(bf16[4,16,64,128]{3,2,1,0:T(8,128)(2,1)} %get-tuple-element.33), calls=%async_computation.2 | async-start | bytes 2097152 | tf_op jit(solution)/shard_map/all_to_all | solution.py:444
  89.5 36.3 %all-to-all-start.3 = ((bf16[16,64,128]{2,1,0:T(8,128)(2,1)}), bf16[16,64,128]{2,1,0:T(8,128)(2,1)S(1)}, u32[]{:S(2)}, u32[]{:S(2)}) async-start(bf16[16,64,128]{2,1,0:T(8,128)(2,1)} %shard_map.142), calls=%async_computation.3 | async-start | bytes 524288 | tf_op jit(solution)/shard_map/all_to_all | solution.py:444
  125.8 33.6 %copy-start.5 = (bf16[64,128]{1,0:T(8,128)(2,1)}, bf16[64,128]{1,0:T(8,128)(2,1)S(1)}, u32[]{:S(2)}) copy-start(bf16[64,128]{1,0:T(8,128)(2,1)S(1)} %add_convert_fusion) | copy-start | bytes 49156
  125.9 4.5 %collective-permute-start.4 = (bf16[32,128]{1,0:T(8,128)(2,1)S(1)}, bf16[32,128]{1,0:T(8,128)(2,1)S(1)}, u32[]{:S(2)}, u32[]{:S(2)}) collective-permute-start(bf16[32,128]{1,0:T(8,128)(2,1)S(1)} %get-tuple-element.65), channel_id=1, source_target_pairs={{0,128},{128,256},{256,384},{1,129},{129,257},{257,385},{2,130},{1... | collective-permute-start | bytes 24584 | tf_op jit(solution)/shard_map/ppermute | solution.py:449
  129.0 4.4 %collective-permute-start.5 = (bf16[32,128]{1,0:T(8,128)(2,1)S(1)}, bf16[32,128]{1,0:T(8,128)(2,1)S(1)}, u32[]{:S(2)}, u32[]{:S(2)}) collective-permute-start(bf16[32,128]{1,0:T(8,128)(2,1)S(1)} %get-tuple-element.64), channel_id=1, source_target_pairs={{128,0},{256,128},{384,256},{129,1},{257,129},{385,257},{130,2},{2... | collective-permute-start | bytes 24584 | tf_op jit(solution)/shard_map/ppermute | solution.py:449
  134.8 23.5 %all-to-all-start.4 = ((bf16[16,64,128]{2,1,0:T(8,128)(2,1)}), bf16[16,64,128]{2,1,0:T(8,128)(2,1)S(1)}, u32[]{:S(2)}, u32[]{:S(2)}) async-start(bf16[16,64,128]{2,1,0:T(8,128)(2,1)} %get-tuple-element.35), calls=%async_computation.4 | async-start | bytes 524288 | tf_op jit(solution)/shard_map/all_to_all | solution.py:444
  145.5 52.5 %collective-permute-start.6 = (bf16[4,16,128,128]{3,2,1,0:T(8,128)(2,1)S(1)}, bf16[4,16,128,128]{3,2,1,0:T(8,128)(2,1)}, u32[]{:S(2)}, u32[]{:S(2)}) collective-permute-start(bf16[4,16,128,128]{3,2,1,0:T(8,128)(2,1)S(1)} %all-to-all-done.1.refs_0_.refs_1_.came0), channel_id=1, source_target_pairs={{0,4},{4,0},{1,5},{5,1},{2,6},{6,2},{3,7},{7,3},{8,12},{12,8},{9,1... | collective-permute-start | bytes 6291464 | tf_op jit(solution)/shard_map/ppermute | solution.py:440
  172.7 6.9 %copy-start.1 = (bf16[4,16,64,128]{3,2,1,0:T(8,128)(2,1)}, bf16[4,16,64,128]{3,2,1,0:T(8,128)(2,1)S(1)}, u32[]{:S(2)}) copy-start(bf16[4,16,64,128]{3,2,1,0:T(8,128)(2,1)S(1)} %all_to_all.45.refs_0_.came1) | copy-start | bytes 3145732
  178.9 0.7 copy-start.2
  179.5 19.7 %collective-permute-start.7 = (bf16[4,16,64,128]{3,2,1,0:T(8,128)(2,1)S(1)}, bf16[4,16,64,128]{3,2,1,0:T(8,128)(2,1)}, u32[]{:S(2)}, u32[]{:S(2)}) collective-permute-start(bf16[4,16,64,128]{3,2,1,0:T(8,128)(2,1)S(1)} %all_to_all.45.refs_0_.came1), channel_id=1, source_target_pairs={{0,4},{4,0},{1,5},{5,1},{2,6},{6,2},{3,7},{7,3},{8,12},{12,8},{9,1... | collective-permute-start | bytes 3145736 | tf_op jit(solution)/shard_map/ppermute | solution.py:440
  189.4 19.5 %all-to-all-start.6 = ((bf16[4,16,64,128]{3,2,1,0:T(8,128)(2,1)}), bf16[4,16,64,128]{3,2,1,0:T(8,128)(2,1)}, u32[]{:S(2)}, u32[]{:S(2)}) async-start(bf16[4,16,64,128]{3,2,1,0:T(8,128)(2,1)} %get-tuple-element.38), calls=%async_computation.6 | async-start | bytes 2097152 | tf_op jit(solution)/shard_map/all_to_all | solution.py:444
  193.7 4.3 %collective-permute-start.8 = (bf16[2,128,224]{2,1,0:T(8,128)(2,1)S(1)}, bf16[2,128,224]{2,1,0:T(8,128)(2,1)S(1)}, u32[]{:S(2)}, u32[]{:S(2)}) collective-permute-start(bf16[2,128,224]{2,1,0:T(8,128)(2,1)S(1)} %get-tuple-element.41), channel_id=1, source_target_pairs={{0,4},{4,0},{1,5},{5,1},{2,6},{6,2},{3,7},{7,3},{8,12},{12,8},{9,1... | collective-permute-start | bytes 344072 | tf_op jit(solution)/shard_map/ppermute | solution.py:440
  195.6 3.6 %collective-permute-start.9 = (bf16[2,128,224]{2,1,0:T(8,128)(2,1)}, bf16[2,128,224]{2,1,0:T(8,128)(2,1)S(1)}, u32[]{:S(2)}, u32[]{:S(2)}) collective-permute-start(bf16[2,128,224]{2,1,0:T(8,128)(2,1)} %copy-done.2), channel_id=1, source_target_pairs={{0,4},{4,0},{1,5},{5,1},{2,6},{6,2},{3,7},{7,3},{8,12},{12,8},{9,1... | collective-permute-start | bytes 344072 | tf_op jit(solution)/shard_map/ppermute | solution.py:440
  199.2 9.7 %copy-start.7 = (f32[4,32]{1,0:T(4,128)S(1)}, f32[4,32]{1,0:T(4,128)}, u32[]{:S(2)}) copy-start(f32[4,32]{1,0:T(4,128)} %get-tuple-element.66) | copy-start | bytes 1540
  203.8 15.3 %copy-start.6 = (bf16[64,128]{1,0:T(8,128)(2,1)S(1)}, bf16[64,128]{1,0:T(8,128)(2,1)}, u32[]{:S(2)}) copy-start(bf16[64,128]{1,0:T(8,128)(2,1)} %copy-done.5) | copy-start | bytes 49156
  211.2 23.0 %all-to-all-start.7 = ((bf16[16,80,128]{2,1,0:T(8,128)(2,1)}), bf16[16,80,128]{2,1,0:T(8,128)(2,1)S(1)}, u32[]{:S(2)}, u32[]{:S(2)}) async-start(bf16[16,80,128]{2,1,0:T(8,128)(2,1)} %shard_map.147), calls=%async_computation.7 | async-start | bytes 655360 | tf_op jit(solution)/shard_map/all_to_all | solution.py:444
  219.2 3.9 %collective-permute-start.3 = (bf16[2,32,64]{2,1,0:T(8,128)(2,1)S(1)}, bf16[2,32,64]{2,1,0:T(8,128)(2,1)S(1)}, u32[]{:S(2)}, u32[]{:S(2)}) collective-permute-start(bf16[2,32,64]{2,1,0:T(8,128)(2,1)S(1)} %get-tuple-element.53), channel_id=1, source_target_pairs={{0,4},{4,0},{1,5},{5,1},{2,6},{6,2},{3,7},{7,3},{8,12},{12,8},{9,1... | collective-permute-start | bytes 24584 | tf_op jit(solution)/shard_map/ppermute | solution.py:440
  235.0 13.4 %collective-permute-start.10 = (bf16[2,32,64]{2,1,0:T(8,128)(2,1)S(1)}, bf16[2,32,64]{2,1,0:T(8,128)(2,1)S(1)}, u32[]{:S(2)}, u32[]{:S(2)}) collective-permute-start(bf16[2,32,64]{2,1,0:T(8,128)(2,1)S(1)} %get-tuple-element.55), channel_id=1, source_target_pairs={{0,4},{4,0},{1,5},{5,1},{2,6},{6,2},{3,7},{7,3},{8,12},{12,8},{9,1... | collective-permute-start | bytes 24584 | tf_op jit(solution)/shard_map/ppermute | solution.py:440
  243.5 12.6 %all-to-all-start.8 = ((f32[32,8,128]{2,1,0:T(8,128)}), f32[32,8,128]{2,1,0:T(8,128)S(1)}, u32[]{:S(2)}, u32[]{:S(2)}) async-start(f32[32,8,128]{2,1,0:T(8,128)} %get-tuple-element.47), calls=%async_computation.8 | async-start | bytes 262144 | tf_op jit(solution)/shard_map/all_to_all | solution.py:444
